TPU v7x, 32 devices: a whole 2x2x4 slice. The times are simulated.
32 devices in a mesh: groups: 2 (over x), seq: 8 (over z, y), section: 2 (over core).
Axes of the slice: x: 2, y: 2, z: 4, core: 2. Of those that a mesh axis runs over, the one named last changes fastest.
Arguments:
- latent_cache: bfloat16 [2, 8, 32768, 576], P('section', 'groups', 'seq'), parts along dimension 1, may hold values from -6 to 6
- index_keys: bfloat16 [2, 8, 32768, 128], P('section', 'groups', 'seq'), parts along dimension 1, may hold values from -6 to 6
- latent_query: bfloat16 [2, 8, 128, 576], P('section', 'groups', 'seq'), parts along dimension 1, may hold values from -54 to 54
- index_query: bfloat16 [2, 8, 64, 128], P('section', 'groups', 'seq'), parts along dimension 1, may hold values from -6 to 6
- index_weight: bfloat16 [2, 8, 64], P('section', 'groups', 'seq'), parts along dimension 1, may hold values from -0.75 to 0.75
- value_up_weight: bfloat16 [2, 128, 512, 128], P('section', 'seq'), may hold values from -0.25 to 0.25
- selected: int32 [2, 8, 2, 32], P('section', 'groups'), parts along dimension 1, may hold values from 0 to 511, as said below
- lengths: int32 [8], P('groups'), parts along dimension 0, may hold values from 16384 to 32767, as said below
Outputs:
- index_scores: float32 [2, 8, 32768], P('section', 'groups', 'seq'), parts along dimension 1
- head_out: bfloat16 [2, 8, 128, 128], P('section', 'groups', 'seq'), parts along dimension 1
There are 2 independent parts, one for each index of `groups`. A program takes and returns all parts, laid end to end along the dimension named above; an argument that names none is the same for every part. Nothing has to cross between parts.
Inputs may be any that keep to these rules, and one draw needn't show every extreme that they name: `lengths`: never one more than a multiple of 64. `selected`: for each layer, row and head group, 32 distinct block numbers, each block starting before the row's length; the block holding the row's last live token is always among them.
All inputs are finite; a program needn't handle non-finite values.
Results may differ from a plain program's by a relative error of at most 0.0048.
Values may be sent and summed in bfloat16 or wider, within the bound.
A program may use at most 128 MiB of HBM per device.

v0:
```python
import functools

import jax
import jax.numpy as jnp
from jax import lax
from jax.experimental import pallas as pl
from jax.experimental.pallas import tpu as pltpu
from jax.sharding import PartitionSpec as P

LATENT_WIDTH = 512
ROTARY_WIDTH = 64
VALUE_WIDTH = 128
IDX_DIM = 128
BLOCK = 64
HEAD_GROUPS = 2
NEG = -1e30
CHUNK = 8
LANES = 128
MESH = pl.DeviceIdType.MESH


def greet_all(n, me):
    barrier = pltpu.get_barrier_semaphore()
    for k in range(1, n):
        pl.semaphore_signal(
            barrier, inc=1, device_id={"seq": lax.rem(me + k, n)}, device_id_type=MESH
        )
    pl.semaphore_wait(barrier, n - 1)


def push(n, me, k, src, dst, send_sem, recv_sem):
    return pltpu.make_async_remote_copy(
        src_ref=src,
        dst_ref=dst,
        send_sem=send_sem.at[k],
        recv_sem=recv_sem.at[k],
        device_id={"seq": lax.rem(me + k, n)},
        device_id_type=MESH,
    )


def gather_kernel(
    n, lens, lq, iq, iw, keys, gq, scores, giq, giw, kbuf,
    key_sem, own_sem, isend, irecv, wsend, wrecv, qsend, qrecv,
):
    me = lax.axis_index("seq")
    rows, span, _ = keys.shape
    half = n // 2
    partner = me + 1 - 2 * lax.rem(me, 2)
    order = sorted(range(1, half), key=lambda k: min(k, half - k))
    loads = []
    for b in range(rows):
        copy = pltpu.make_async_copy(keys.at[b], kbuf.at[b], key_sem.at[b])
        copy.start()
        loads.append(copy)
    own = [
        pltpu.make_async_copy(iq, giq.at[me], own_sem.at[0]),
        pltpu.make_async_copy(iw, giw.at[me], own_sem.at[1]),
        pltpu.make_async_copy(lq, gq.at[me], own_sem.at[2]),
    ]
    for copy in own:
        copy.start()
    greet_all(n, me)

    def push(peer, k, src, dst, send_sem, recv_sem):
        return pltpu.make_async_remote_copy(
            src_ref=src,
            dst_ref=dst,
            send_sem=send_sem.at[k],
            recv_sem=recv_sem.at[k],
            device_id={"seq": peer},
            device_id_type=MESH,
        )

    def first_hop(src, dst, send_sem, recv_sem):
        away = {
            k: push(lax.rem(me + 2 * k, n), k, src, dst.at[me], send_sem, recv_sem)
            for k in order
        }
        return away, push(partner, half, src, dst.at[me], send_sem, recv_sem)

    def second_hop(dst, send_sem, recv_sem):
        passed = {}
        for k in order:
            owner = lax.rem(me - 2 * k + n, n)
            passed[k] = push(
                partner, half + k, dst.at[owner], dst.at[owner], send_sem, recv_sem
            )
        return passed

    small = []
    for k in range(1, n):
        peer = lax.rem(me + k, n)
        small.append(push(peer, k, iq, giq.at[me], isend, irecv))
        small.append(push(peer, k, iw, giw.at[me], wsend, wrecv))
    (large, large_pair), large_on = first_hop(lq, gq, qsend, qrecv), second_hop(gq, qsend, qrecv)
    for copy in small:
        copy.start()
    for k in order:
        large[k].start()
    large_pair.start()
    for copy in loads:
        copy.wait()
    own[0].wait()
    own[1].wait()
    for copy in small:
        copy.wait_recv()
    tile = min(512, span)
    lane = lax.broadcasted_iota(jnp.int32, (1, tile), 1)
    held = giq.shape[2]
    given = iw.shape[1]
    diagonal = (
        lax.broadcasted_iota(jnp.int32, (n * held, given), 0) % held
        == lax.broadcasted_iota(jnp.int32, (n * held, given), 1)
    )
    waiting = list(order)
    for b in range(rows):
        query = giq[:, b].astype(jnp.float32).reshape(n * held, giq.shape[3])
        query = query.astype(jnp.bfloat16)
        weight = giw[:, b : b + 1].astype(jnp.float32)
        weight = jnp.broadcast_to(weight, (n, held, given)).reshape(n * held, given)
        weight = jnp.sum(jnp.where(diagonal, weight, 0.0), axis=1, keepdims=True)
        weight = jnp.broadcast_to(weight * IDX_DIM ** (-0.5), (n * held, LANES))
        length = lens[b]

        def step(c, carry, b=b, query=query, weight=weight, length=length):
            start = pl.multiple_of(c * tile, tile)
            dots = lax.dot_general(
                query,
                kbuf[b, pl.ds(start, tile), :],
                (((1,), (1,)), ((), ())),
                preferred_element_type=jnp.float32,
            )
            pieces = []
            for j in range(tile // LANES):
                part = jnp.maximum(dots[:, j * LANES : (j + 1) * LANES], 0.0) * weight
                pieces.append(jnp.sum(part, axis=0, keepdims=True))
            total = jnp.concatenate(pieces, axis=1)
            live = me * span + c * tile + lane < length
            scores[b : b + 1, pl.ds(start, tile)] = jnp.where(live, total, 0.0)
            return carry

        lax.fori_loop(0, span // tile, step, 0)
        if waiting:
            k = waiting.pop(0)
            large[k].wait_recv()
            large_on[k].start()
    for k in waiting:
        large[k].wait_recv()
        large_on[k].start()
    own[2].wait()
    large_pair.wait_recv()
    for k in order:
        large_on[k].wait_recv()
    for copy in small:
        copy.wait_send()
    large_pair.wait_send()
    for k in order:
        large[k].wait_send()
        large_on[k].wait_send()


def local_kernel(sel, lens, gq, cache, parts, stats, buf, counts, kept, sems):
    me = lax.axis_index("seq")
    rows, width, span = cache.shape
    nsel = sel.shape[2]
    here = span // BLOCK
    first = me * here

    def block_copy(b, rg, block, slot):
        start = pl.multiple_of((block - first) // 2 * LANES, LANES)
        dest = pl.multiple_of(slot * LANES, LANES)
        return pltpu.make_async_copy(
            cache.at[b, :, pl.ds(start, LANES)],
            buf.at[rg, :, pl.ds(dest, LANES)],
            sems.at[rg, slot],
        )

    for b in range(rows):
        for g in range(HEAD_GROUPS):
            rg = b * HEAD_GROUPS + g

            def scan(i, slot, b=b, g=g, rg=rg):
                block = sel[b, g, i]
                kept[rg, slot] = block
                mine = jnp.logical_and(block >= first, block < first + here)
                return slot + mine.astype(jnp.int32)

            count = lax.fori_loop(0, nsel, scan, jnp.int32(0), unroll=True)
            counts[rg] = count

            @pl.loop(0, count)
            def _(slot, b=b, rg=rg):
                block_copy(b, rg, kept[rg, slot], slot).start()

    for rg in range(rows * HEAD_GROUPS):
        count = counts[rg]

        @pl.loop(count, jnp.maximum((count + CHUNK - 1) // CHUNK, 1) * CHUNK)
        def _(slot, rg=rg):
            dest = pl.multiple_of(slot * LANES, LANES)
            buf[rg, :, pl.ds(dest, LANES)] = jnp.zeros((width, LANES), jnp.bfloat16)

    heads = gq.shape[2]
    per_group = gq.shape[0] // HEAD_GROUPS
    group_wise = per_group * heads
    tokens = CHUNK * LANES
    scale = (VALUE_WIDTH + ROTARY_WIDTH) ** (-0.5)
    lane = lax.broadcasted_iota(jnp.int32, (1, LANES), 1)
    for g in range(HEAD_GROUPS):
        table = jnp.zeros((group_wise, LANES), jnp.float32)
        for b in range(rows):
            rg = b * HEAD_GROUPS + g
            count = counts[rg]
            steps = jnp.maximum((count + CHUNK - 1) // CHUNK, 1)

            @pl.loop(0, count)
            def _(slot, b=b, rg=rg):
                block_copy(b, rg, first, slot).wait()

            query = gq[g * per_group : (g + 1) * per_group, b].reshape(group_wise, width)

            def chunk(c, b=b, rg=rg, query=query, count=count):
                base = pl.multiple_of(c * tokens, tokens)
                s = jnp.dot(
                    query,
                    buf[rg, :, pl.ds(base, tokens)],
                    preferred_element_type=jnp.float32,
                ) * scale
                bounds = []
                for j in range(CHUNK):
                    slot = c * CHUNK + j
                    block = kept[rg, slot]
                    begin = block % 2 * BLOCK
                    live = jnp.minimum(BLOCK, lens[b] - block * BLOCK)
                    bounds.append((begin, jnp.where(slot < count, begin + live, 0)))
                usable = jnp.concatenate(
                    [
                        ((lane >= lo) & (lane < hi)).astype(jnp.int32)
                        for lo, hi in bounds
                    ],
                    axis=1,
                ) > 0
                s = jnp.where(usable, s, NEG)
                return s, usable, buf[rg, :LATENT_WIDTH, pl.ds(base, tokens)]

            def mix(p, values):
                return lax.dot_general(
                    p.astype(jnp.bfloat16),
                    values,
                    (((1,), (1,)), ((), ())),
                    preferred_element_type=jnp.float32,
                )

            s, usable, values = chunk(0)
            top = jnp.max(s, axis=1, keepdims=True)
            p = jnp.where(usable, jnp.exp(s - top), 0.0)
            total = jnp.sum(p, axis=1, keepdims=True)
            acc = mix(p, values)

            def more(c, carry, chunk=chunk):
                top, total, acc = carry
                s, usable, values = chunk(c)
                new = jnp.maximum(top, jnp.max(s, axis=1, keepdims=True))
                p = jnp.where(usable, jnp.exp(s - new), 0.0)
                keep = jnp.exp(top - new)
                total = total * keep + jnp.sum(p, axis=1, keepdims=True)
                return new, total, acc * keep + mix(p, values)

            top, total, acc = lax.fori_loop(1, steps, more, (top, total, acc))
            parts[g * per_group : (g + 1) * per_group, b] = acc.astype(jnp.bfloat16).reshape(
                per_group, heads, LATENT_WIDTH
            )
            table = jnp.where(lane == 2 * b, top, table)
            table = jnp.where(lane == 2 * b + 1, total, table)
        stats[g * per_group : (g + 1) * per_group] = table.reshape(per_group, heads, LANES)


def exchange_kernel(
    n, parts, stats, weight, out, rparts, rstats, wbuf,
    own_sem, psend, precv, ssend, srecv,
):
    me = lax.axis_index("seq")
    _, rows, heads, latent = parts.shape
    own = [
        pltpu.make_async_copy(weight, wbuf, own_sem.at[0]),
        pltpu.make_async_copy(parts.at[me], rparts.at[me], own_sem.at[1]),
        pltpu.make_async_copy(stats.at[me], rstats.at[me], own_sem.at[2]),
    ]
    for copy in own:
        copy.start()
    greet_all(n, me)
    sends = []
    for k in range(1, n):
        peer = lax.rem(me + k, n)
        sends.append(push(n, me, k, stats.at[peer], rstats.at[me], ssend, srecv))
        sends.append(push(n, me, k, parts.at[peer], rparts.at[me], psend, precv))
    for copy in sends:
        copy.start()
    for copy in own:
        copy.wait()
    for copy in sends:
        copy.wait_recv()
    table = rstats[...]
    attended = []
    for b in range(rows):
        tops = [table[s, :, 2 * b : 2 * b + 1] for s in range(n)]
        joint = functools.reduce(jnp.maximum, tops)
        total = jnp.zeros_like(joint)
        acc = jnp.zeros((heads, latent), jnp.float32)
        for s in range(n):
            factor = jnp.exp(tops[s] - joint)
            total = total + factor * table[s, :, 2 * b + 1 : 2 * b + 2]
            acc = acc + factor * rparts[s, b].astype(jnp.float32)
        attended.append(acc / total)
    attended = jnp.concatenate(attended, axis=0).astype(jnp.bfloat16)
    which = lax.broadcasted_iota(jnp.int32, (rows * heads, 1), 0) % heads

    def project(h, acc):
        y = jnp.dot(attended, wbuf[h], preferred_element_type=jnp.float32)
        return jnp.where(which == h, y, acc)

    y = jnp.zeros((rows * heads, weight.shape[2]), jnp.float32)
    y = lax.fori_loop(0, heads, project, y, unroll=4)
    out[...] = y.reshape(rows, heads, weight.shape[2]).astype(out.dtype)
    for copy in sends:
        copy.wait_send()


def on_device(
    n,
    latent_cache,
    index_keys,
    latent_query,
    index_query,
    index_weight,
    value_up_weight,
    selected,
    lengths,
):
    cache, keys, lq = latent_cache[0], index_keys[0], latent_query[0]
    iq, iw, weight, sel = index_query[0], index_weight[0], value_up_weight[0], selected[0]
    rows, span, width = cache.shape
    heads = lq.shape[1]
    extra = -iq.shape[1] % 8
    if extra:
        iq = jnp.pad(iq, ((0, 0), (0, extra), (0, 0)))
    vmem = pl.BlockSpec(memory_space=pltpu.VMEM)
    smem = pl.BlockSpec(memory_space=pltpu.SMEM)
    hbm = pl.BlockSpec(memory_space=pl.ANY)
    dma = pltpu.SemaphoreType.DMA
    limit = 60 * 1024 * 1024

    gq, index_scores = pl.pallas_call(
        functools.partial(gather_kernel, n),
        out_shape=(
            jax.ShapeDtypeStruct((n,) + lq.shape, lq.dtype),
            jax.ShapeDtypeStruct((rows, span), jnp.float32),
        ),
        in_specs=[smem, vmem, vmem, vmem, hbm],
        out_specs=(hbm, vmem),
        scratch_shapes=[
            pltpu.VMEM((n,) + iq.shape, iq.dtype),
            pltpu.VMEM((n,) + iw.shape, iw.dtype),
            pltpu.VMEM(keys.shape, keys.dtype),
            dma((rows,)), dma((3,)), dma((n,)), dma((n,)), dma((n,)), dma((n,)),
            dma((n,)), dma((n,)),
        ],
        compiler_params=pltpu.CompilerParams(
            collective_id=0, has_side_effects=True, vmem_limit_bytes=limit
        ),
        name="gather",
    )(lengths, lq, iq, iw, keys)

    whole_heads = n * heads
    if heads % 16:
        gq = gq.transpose(1, 0, 2, 3).reshape(
            rows, HEAD_GROUPS, whole_heads // HEAD_GROUPS, width
        ).transpose(1, 0, 2, 3)
    slots = gq.shape[0]
    wide = gq.shape[2]
    pairs = rows * HEAD_GROUPS
    nsel = sel.shape[2]
    room = -(-nsel // CHUNK) * CHUNK
    parts, stats = pl.pallas_call(
        local_kernel,
        out_shape=(
            jax.ShapeDtypeStruct((slots, rows, wide, LATENT_WIDTH), jnp.bfloat16),
            jax.ShapeDtypeStruct((slots, wide, 128), jnp.float32),
        ),
        in_specs=[smem, smem, vmem, hbm],
        out_specs=(vmem, vmem),
        scratch_shapes=[
            pltpu.VMEM((pairs, width, room * LANES), cache.dtype),
            pltpu.SMEM((pairs,), jnp.int32),
            pltpu.SMEM((pairs, room), jnp.int32),
            dma((pairs, nsel)),
        ],
        compiler_params=pltpu.CompilerParams(vmem_limit_bytes=limit),
        name="local",
    )(sel, lengths, gq, jnp.swapaxes(cache, 1, 2))
    if slots != n:
        parts = parts.transpose(1, 0, 2, 3).reshape(rows, n, heads, LATENT_WIDTH)
        parts = parts.transpose(1, 0, 2, 3)
        stats = stats.reshape(n, heads, 128)

    head_out = pl.pallas_call(
        functools.partial(exchange_kernel, n),
        out_shape=jax.ShapeDtypeStruct((rows, heads, weight.shape[2]), jnp.float32),
        in_specs=[hbm, hbm, hbm],
        out_specs=vmem,
        scratch_shapes=[
            pltpu.VMEM(parts.shape, parts.dtype),
            pltpu.VMEM(stats.shape, stats.dtype),
            pltpu.VMEM(weight.shape, weight.dtype),
            dma((3,)), dma((n,)), dma((n,)), dma((n,)), dma((n,)),
        ],
        compiler_params=pltpu.CompilerParams(
            collective_id=1, has_side_effects=True, vmem_limit_bytes=limit
        ),
        name="exchange",
    )(parts, stats, weight)
    return (index_scores[None], head_out.astype(jnp.bfloat16)[None])


def solution(mesh):
    return jax.shard_map(
        functools.partial(on_device, mesh.shape["seq"]),
        mesh=mesh,
        in_specs=(
            P("section", "groups", "seq", None),
            P("section", "groups", "seq", None),
            P("section", "groups", "seq", None),
            P("section", "groups", "seq", None),
            P("section", "groups", "seq"),
            P("section", "seq", None, None),
            P("section", "groups", None, None),
            P("groups"),
        ),
        out_specs=(P("section", "groups", "seq"), P("section", "groups", "seq", None)),
        check_vma=False,
    )
```

profile of v0, /device:TPU:14, one launch (start us, length us, event | category | flops | bytes accessed | tf_op | source)
XLA Modules:
  0.0 53.9 jit_solution(14073561058366724819)
XLA Ops:
  0.6 18.8 %gather.1 = (bf16[8,4,16,576]{3,2,1,0:T(8,128)(2,1)}, f32[4,4096]{1,0:T(4,128)}) custom-call(s32[4]{0:T(128)} %lens.3, bf16[4,16,576]{2,1,0:T(8,128)(2,1)} %bitcast.15, bf16[4,8,128]{2,1,0:T(8,128)(2,1)} %bitcast.17, bf16[4,8]{1,0:T(4,128)(2,1)} %bitcast.19, bf16[4,4096,128]{2,1,0:T(8,128)(2,1)} %bitcast.13), custom_call_target="tpu_custom_call" | custom-call | tf_op jit(solution)/shard_map/gather/pallas_call | solution.py:354
  19.5 0.0 copy-start
  19.5 13.5 %local.1 = (bf16[8,4,16,512]{3,2,1,0:T(8,128)(2,1)}, f32[8,16,128]{2,1,0:T(8,128)}) custom-call(s32[4,2,32]{2,1,0:T(2,128)} %bitcast.18, s32[4]{0:T(128)} %lens.3, bf16[8,4,16,576]{3,2,1,0:T(8,128)(2,1)} %get-tuple-element.7.gq, bf16[4,576,4096]{2,1,0:T(8,128)(2,1)} %bitcast.12), custom_call_target="tpu_custom_call" | custom-call | tf_op jit(solution)/shard_map/local/pallas_call | solution.py:385
  33.0 19.0 %exchange.1 = f32[4,16,128]{2,1,0:T(8,128)} custom-call(bf16[8,4,16,512]{3,2,1,0:T(8,128)(2,1)} %get-tuple-element.8.parts, f32[8,16,128]{2,1,0:T(8,128)} %get-tuple-element.9.stats, bf16[16,512,128]{2,1,0:T(8,128)(2,1)} %bitcast.14), custom_call_target="tpu_custom_call" | custom-call | tf_op jit(solution)/shard_map/exchange/pallas_call | solution.py:407
  51.9 1.4 %convert_bitcast_fusion = bf16[1,4,16,128]{3,2,1,0:T(8,128)(2,1)} fusion(f32[4,16,128]{2,1,0:T(8,128)} %exchange.1), kind=kLoop, calls=%fused_computation | loop fusion | flops 8192 | bytes 49152 | tf_op jit(solution)/shard_map/broadcast_in_dim | solution.py:423
  53.3 0.0 copy-done
  53.3 0.6 %copy.11 = f32[1,4,4096]{2,1,0:T(4,128)} copy(f32[1,4,4096]{2,1,0:T(4,128)S(1)} %bitcast.16) | data formatting | bytes 131072
Async XLA Ops:
  19.5 33.8 %copy-start = (f32[4,4096]{1,0:T(4,128)S(1)}, f32[4,4096]{1,0:T(4,128)}, u32[]{:S(2)}) copy-start(f32[4,4096]{1,0:T(4,128)} %get-tuple-element.6) | copy-start | bytes 196612
where the time goes:
time: 54.5 us; the launch traced here: 53.9 us
  Pallas kernels  51.3 us (94%)
  other arithmetic  1.37 us (3%)
  between operations  0.66 us (1%)
  local copies, waits for them, and re-layouts  0.63 us (1%)
    pallas_call x1, Pallas kernels, on_device(): pl.pallas_call(functools.partial(exchange_kernel, n), out_shape=jax.Shape...  19 us
    pallas_call x1, Pallas kernels, on_device(): pl.pallas_call(functools.partial(gather_kernel, n), out_shape=(jax.ShapeD...  18.8 us
    pallas_call x1, Pallas kernels, on_device(): pl.pallas_call(local_kernel, out_shape=(jax.ShapeDtypeStruct((slots, rows...  13.5 us
    broadcast_in_dim x1, other arithmetic, on_device(): return (index_scores[None], head_out.astype(jnp.bfloat16)[None])  1.37 us

commit v1 on v0

v1 whole, which is shorter than its diff:
```python
import functools

import jax
import jax.numpy as jnp
from jax import lax
from jax.experimental import pallas as pl
from jax.experimental.pallas import tpu as pltpu
from jax.sharding import PartitionSpec as P

LATENT_WIDTH = 512
ROTARY_WIDTH = 64
VALUE_WIDTH = 128
IDX_DIM = 128
BLOCK = 64
HEAD_GROUPS = 2
NEG = -1e30
LOG2E = 1.4426950408889634
FIRST = 8
MORE = 4
LANES = 128
PACKED = LATENT_WIDTH + LANES
MIB = 1024 * 1024
MESH = pl.DeviceIdType.MESH


class Line:
    def __init__(self, n):
        self.half = n // 2
        self.me = lax.axis_index("seq")
        self.z = lax.div(self.me, 2)
        self.y = lax.rem(self.me, 2)
        self.partner = self.me + 1 - 2 * self.y
        self.order = sorted(range(1, self.half), key=lambda k: (-k.bit_length(), k))

    def step(self, k, sign):
        if self.half & (self.half - 1):
            return lax.rem(self.z + sign * k + self.half, self.half)
        out = self.z
        for j in range(k.bit_length()):
            if k >> j & 1:
                bit = lax.rem(lax.div(self.z, 1 << j), 2)
                out = out + (1 - 2 * bit) * (1 << j)
        return out

    def to(self, k):
        return self.step(k, 1)

    def frm(self, k):
        return self.step(k, -1)

    def device(self, z):
        return 2 * z + self.y

    def greet(self):
        barrier = pltpu.get_barrier_semaphore()
        peers = [self.partner] + [self.device(self.to(k)) for k in self.order]
        for peer in peers:
            pl.semaphore_signal(
                barrier, inc=1, device_id={"seq": peer}, device_id_type=MESH
            )
        return lambda: pl.semaphore_wait(barrier, self.half)


def push(peer, src, dst, send_sem, recv_sem):
    return pltpu.make_async_remote_copy(
        src_ref=src,
        dst_ref=dst,
        send_sem=send_sem,
        recv_sem=recv_sem,
        device_id={"seq": peer},
        device_id_type=MESH,
    )


def gather_kernel(
    n, lq, iq, iw, sel, keys, weight, gq, giw, kbuf, wbuf, table,
    lqs, iqs, sels, load_sem, zsend, zrecv, ysend, yrecv,
):
    line = Line(n)
    me = line.me
    rows, heads, width = lqs.shape
    held = iw.shape[1]
    entered = line.greet()
    loads = [
        pltpu.make_async_copy(lq, lqs, load_sem.at[0]),
        pltpu.make_async_copy(iq, iqs, load_sem.at[1]),
        pltpu.make_async_copy(iw, giw.at[me], load_sem.at[2]),
        pltpu.make_async_copy(sel, sels, load_sem.at[3]),
        pltpu.make_async_copy(keys, kbuf, load_sem.at[4]),
        pltpu.make_async_copy(weight, wbuf, load_sem.at[5]),
    ]
    for copy in loads:
        copy.start()
    for copy in loads[:3]:
        copy.wait()

    lane = lax.broadcasted_iota(jnp.int32, (iqs.shape[1], LANES), 1)
    row = lax.broadcasted_iota(jnp.int32, (iqs.shape[1], LANES), 0)
    for b in range(rows):
        mine = iqs[b].astype(jnp.float32)
        turned = pltpu.roll(mine, LANES // 2, 1)
        if heads == 2 * iqs.shape[1]:
            spare = jnp.concatenate([turned, mine], axis=0)
        else:
            spare = jnp.where(row < held, turned, pltpu.roll(mine, held, 0))
        gq[me, b, :, 0:LATENT_WIDTH] = lqs[b, :, 0:LATENT_WIDTH]
        gq[me, b, :, LATENT_WIDTH:width] = lqs[b, :, LATENT_WIDTH:width]
        spare = spare.astype(jnp.bfloat16)
        gq[me, b, :, width:PACKED] = spare[:, width - LATENT_WIDTH :]
    entered()

    def pieces(owner):
        return [gq.at[owner, b] for b in range(rows)] + [giw.at[owner]]

    across, along, onward = [], {}, {}
    for r, ref in enumerate(pieces(me)):
        across.append(push(line.partner, ref, ref, ysend.at[0, r], yrecv.at[0, r]))
        for k in line.order:
            along[k, r] = push(
                line.device(line.to(k)), ref, ref, zsend.at[k, r], zrecv.at[k, r]
            )
    for k in line.order:
        for r, ref in enumerate(pieces(line.device(line.frm(k)))):
            onward[k, r] = push(line.partner, ref, ref, ysend.at[k, r], yrecv.at[k, r])
    for r in range(rows, -1, -1):
        for k in line.order:
            along[k, r].start()
        across[r].start()

    loads[3].wait()
    here = keys.shape[1] // BLOCK
    first = me * here
    chosen = sels[...]
    spots = lax.broadcasted_iota(jnp.int32, table.shape, 2)
    kept = jnp.full(table.shape, -1, jnp.int32)
    count = jnp.zeros(table.shape, jnp.int32)
    for i in range(sels.shape[2]):
        block = jnp.broadcast_to(chosen[:, :, i : i + 1], table.shape)
        mine = (block >= first) & (block < first + here)
        kept = jnp.where(mine & (spots == count), block, kept)
        count = count + jnp.where(mine, 1, 0)
    table[...] = jnp.where(spots == LANES - 1, count, kept)

    for r in range(rows, -1, -1):
        for k in line.order:
            along[k, r].wait_recv()
            onward[k, r].start()
    loads[4].wait()
    loads[5].wait()
    for r in range(rows, -1, -1):
        across[r].wait_recv()
        for k in line.order:
            onward[k, r].wait_recv()
    for r in range(rows, -1, -1):
        across[r].wait_send()
        for k in line.order:
            along[k, r].wait_send()
            onward[k, r].wait_send()


def local_kernel(table, lens, gq, cache, own, sent, own_lse, sent_lse, buf, sems):
    me = lax.axis_index("seq")
    side = lax.rem(me, 2)
    rows, width, span = cache.shape
    here = span // BLOCK
    first = me * here
    pairs = rows * HEAD_GROUPS

    def count_of(b, g):
        return table[b, g, LANES - 1]

    def block_copy(b, g, block, slot):
        rg = b * HEAD_GROUPS + g
        start = pl.multiple_of((block - first) // 2 * LANES, LANES)
        dest = pl.multiple_of(slot * LANES, LANES)
        return pltpu.make_async_copy(
            cache.at[b, :, pl.ds(start, LANES)],
            buf.at[rg, :, pl.ds(dest, LANES)],
            sems.at[rg, slot],
        )

    @pl.loop(0, pairs)
    def _(rg):
        b, g = rg // HEAD_GROUPS, rg % HEAD_GROUPS

        @pl.loop(0, count_of(b, g))
        def _(slot):
            block_copy(b, g, table[b, g, slot], slot).start()

    @pl.loop(0, pairs)
    def _(rg):
        count = count_of(rg // HEAD_GROUPS, rg % HEAD_GROUPS)
        extra = jnp.maximum(count - FIRST, 0)
        room = FIRST + (extra + MORE - 1) // MORE * MORE

        @pl.loop(count, room)
        def _(slot):
            dest = pl.multiple_of(slot * LANES, LANES)
            buf[rg, :, pl.ds(dest, LANES)] = jnp.zeros((width, LANES), jnp.bfloat16)

    heads = gq.shape[2]
    per_group = gq.shape[0] // HEAD_GROUPS
    wide = per_group * heads
    scale = (VALUE_WIDTH + ROTARY_WIDTH) ** (-0.5) * LOG2E
    lane = lax.broadcasted_iota(jnp.int32, (1, LANES), 1)
    spot = lax.broadcasted_iota(jnp.int32, (per_group // 2, heads, LANES), 2)

    def scores(b, g, query, base, slots):
        rg = b * HEAD_GROUPS + g
        count = count_of(b, g)
        bias = []
        for j in range(slots):
            slot = base + j
            block = table[b, g, slot]
            begin = block % 2 * BLOCK
            live = jnp.minimum(BLOCK, lens[b] - block * BLOCK)
            end = jnp.where(slot < count, begin + live, 0)
            bias.append(jnp.where((lane >= begin) & (lane < end), 0.0, NEG))
        bias = jnp.concatenate(bias, axis=1)
        start = base * LANES
        if not isinstance(start, int):
            start = pl.multiple_of(start, MORE * LANES)
        window = pl.ds(start, slots * LANES)
        s = jnp.dot(query, buf[rg, :, window], preferred_element_type=jnp.float32)
        return s * scale + bias, window

    def mix(b, g, p, window):
        return lax.dot_general(
            p.astype(jnp.bfloat16),
            buf[b * HEAD_GROUPS + g, :LATENT_WIDTH, window],
            (((1,), (1,)), ((), ())),
            preferred_element_type=jnp.float32,
        )

    @pl.loop(0, rows)
    def _(b):
        for g in range(HEAD_GROUPS):

            @pl.loop(0, count_of(b, g))
            def _(slot, g=g):
                block_copy(b, g, first, slot).wait()

        queries, state = [], []
        for g in range(HEAD_GROUPS):
            query = gq[pl.ds(g * per_group, per_group), b]
            if heads % 16:
                query = query.astype(jnp.float32)
            query = query.reshape(wide, PACKED)[:, :width].astype(jnp.bfloat16)
            queries.append(query)
        firsts = [scores(b, g, queries[g], 0, FIRST) for g in range(HEAD_GROUPS)]
        for g, (s, window) in enumerate(firsts):
            top = jnp.max(s, axis=1, keepdims=True)
            p = jnp.exp2(s - top)
            state.append((top, jnp.sum(p, axis=1, keepdims=True), mix(b, g, p, window)))

        for g in range(HEAD_GROUPS):

            def more(c, carry, g=g):
                top, total, acc = carry
                s, window = scores(b, g, queries[g], FIRST + c * MORE, MORE)
                new = jnp.maximum(top, jnp.max(s, axis=1, keepdims=True))
                p = jnp.exp2(s - new)
                keep = jnp.exp2(top - new)
                total = total * keep + jnp.sum(p, axis=1, keepdims=True)
                return new, total, acc * keep + mix(b, g, p, window)

            extra = jnp.maximum(count_of(b, g) - FIRST, 0)
            top, total, acc = lax.fori_loop(0, (extra + MORE - 1) // MORE, more, state[g])
            acc = (acc / total).reshape(per_group, heads, LATENT_WIDTH)
            lse = jnp.broadcast_to(top + jnp.log2(total), (wide, LANES))
            lse = lse.reshape(per_group, heads, LANES)
            acc = acc.reshape(per_group // 2, 2, heads, LATENT_WIDTH)
            lse = lse.reshape(per_group // 2, 2, heads, LANES)
            here_z = pl.ds(g * per_group // 2, per_group // 2)
            even = side == 0
            own[here_z, b] = jnp.where(even, acc[:, 0], acc[:, 1])
            sent[here_z, b] = jnp.where(even, acc[:, 1], acc[:, 0]).astype(jnp.bfloat16)
            own_lse[here_z] = jnp.where(
                spot == b, jnp.where(even, lse[:, 0], lse[:, 1]), own_lse[here_z]
            )
            sent_lse[here_z] = jnp.where(
                spot == b, jnp.where(even, lse[:, 1], lse[:, 0]), sent_lse[here_z]
            )


def exchange_kernel(
    n, lens, own, sent, own_lse, sent_lse, gq, giw, kbuf, attended, scores,
    kept, from_pair, pair_lse, joint, joint_lse, from_line, line_lse,
    ysend, yrecv, zsend, zrecv,
):
    line = Line(n)
    half, me = line.half, line.me
    _, rows, heads, latent = own.shape
    entered = line.greet()
    entered()

    ring = line.order + [0]
    across, along = {}, {}
    for k in ring:
        z = line.to(k)
        refs = [(sent_lse.at[z], pair_lse.at[z])]
        refs += [(sent.at[z, b], from_pair.at[z, b]) for b in range(rows)]
        for r, (src, dst) in enumerate(refs):
            across[k, r] = push(line.partner, src, dst, ysend.at[k, r], yrecv.at[k, r])
            across[k, r].start()

    span = kbuf.shape[1]
    tile = min(512, span)
    lane = lax.broadcasted_iota(jnp.int32, (1, tile), 1)
    held = giw.shape[2]
    group = 8
    diagonal = (
        lax.broadcasted_iota(jnp.int32, (n * group, held), 0) % group
        == lax.broadcasted_iota(jnp.int32, (n * group, held), 1)
    )
    low = lax.broadcasted_iota(jnp.int32, (n * group, LANES), 1) < LANES // 2

    def index_row(b):
        packed = gq[:, b, :, LATENT_WIDTH:PACKED].astype(jnp.float32)
        if heads == 2 * group:
            left = packed[:, :group].reshape(n * group, LANES)
            right = packed[:, group:].reshape(n * group, LANES)
        else:
            left = packed.reshape(n * group, LANES)
            right = pltpu.roll(left, n * group - held, 0)
        query = jnp.where(low, pltpu.roll(left, LANES // 2, 1), right)
        query = query.astype(jnp.bfloat16)
        weight = giw[:, b : b + 1].astype(jnp.float32)
        weight = jnp.broadcast_to(weight, (n, group, held)).reshape(n * group, held)
        weight = jnp.sum(jnp.where(diagonal, weight, 0.0), axis=1, keepdims=True)
        weight = jnp.broadcast_to(weight * IDX_DIM ** (-0.5), (n * group, LANES))
        length = lens[b]

        def step(c, carry):
            start = pl.multiple_of(c * tile, tile)
            dots = lax.dot_general(
                query,
                kbuf[b, pl.ds(start, tile), :],
                (((1,), (1,)), ((), ())),
                preferred_element_type=jnp.float32,
            )
            pieces = []
            for j in range(tile // LANES):
                part = jnp.maximum(dots[:, j * LANES : (j + 1) * LANES], 0.0) * weight
                pieces.append(jnp.sum(part, axis=0, keepdims=True))
            total = jnp.concatenate(pieces, axis=1)
            live = me * span + c * tile + lane < length
            scores[b : b + 1, pl.ds(start, tile)] = jnp.where(live, total, 0.0)
            return carry

        lax.fori_loop(0, span // tile, step, 0)

    def weigh(parts):
        best = functools.reduce(jnp.maximum, parts)
        grown = [jnp.exp2(part - best) for part in parts]
        whole = functools.reduce(jnp.add, grown)
        return [part / whole for part in grown], best + jnp.log2(whole)

    early = rows // 2
    for b in range(early):
        index_row(b)

    for k in ring:
        z = line.to(k)
        across[k, 0].wait_recv()
        (mine, theirs), lse = weigh([own_lse[z], pair_lse[z]])
        if k:
            joint_lse[z] = lse
            target = line.device(z)
            along[k, 0] = push(
                target, joint_lse.at[z], line_lse.at[line.z], zsend.at[k, 0], zrecv.at[k, 0]
            )
        else:
            line_lse[z] = lse
        for b in range(rows):
            across[k, b + 1].wait_recv()
            value = mine[:, b : b + 1] * own[z, b]
            value += theirs[:, b : b + 1] * from_pair[z, b].astype(jnp.float32)
            if k:
                joint[z, b] = value.astype(jnp.bfloat16)
                along[k, b + 1] = push(
                    target, joint.at[z, b], from_line.at[line.z, b],
                    zsend.at[k, b + 1], zrecv.at[k, b + 1],
                )
            else:
                kept[b] = value
        if k:
            for r in range(rows + 1):
                along[k, r].start()

    for b in range(early, rows):
        index_row(b)

    for k in line.order:
        along[k, 0].wait_recv()
    spans = [line.z] + [line.frm(k) for k in line.order]
    factors, _ = weigh([line_lse[z] for z in spans])
    for b in range(rows):
        for k in line.order:
            along[k, b + 1].wait_recv()
        value = factors[0][:, b : b + 1] * kept[b]
        for z, factor in zip(spans[1:], factors[1:]):
            value += factor[:, b : b + 1] * from_line[z, b].astype(jnp.float32)
        attended[b] = value.astype(attended.dtype)
    for copy in list(across.values()) + list(along.values()):
        copy.wait_send()


def project_kernel(attended, weight, scores, out, scores_out, sem):
    copy = pltpu.make_async_copy(scores, scores_out, sem.at[0])
    copy.start()
    rows, heads, latent = attended.shape
    flat = attended[...]
    if heads % 16:
        flat = flat.astype(jnp.float32)
    flat = flat.reshape(rows * heads, latent).astype(jnp.bfloat16)
    which = lax.broadcasted_iota(jnp.int32, (rows * heads, 1), 0) % heads
    y = jnp.zeros((rows * heads, weight.shape[2]), jnp.float32)
    for h in range(heads):
        part = jnp.dot(flat, weight[h], preferred_element_type=jnp.float32)
        y = jnp.where(which == h, part, y)
    out[...] = y.reshape(rows, heads, weight.shape[2]).astype(out.dtype)
    copy.wait()


def on_device(
    n,
    latent_cache,
    index_keys,
    latent_query,
    index_query,
    index_weight,
    value_up_weight,
    selected,
    lengths,
):
    cache, keys, lq = latent_cache[0], index_keys[0], latent_query[0]
    iq, iw, weight, sel = index_query[0], index_weight[0], value_up_weight[0], selected[0]
    rows, span, width = cache.shape
    heads = lq.shape[1]
    half = n // 2
    extra = -iq.shape[1] % 8
    if extra:
        iq = jnp.pad(iq, ((0, 0), (0, extra), (0, 0)))
    vmem = pl.BlockSpec(memory_space=pltpu.VMEM)
    smem = pl.BlockSpec(memory_space=pltpu.SMEM)
    hbm = pl.BlockSpec(memory_space=pl.ANY)
    dma = pltpu.SemaphoreType.DMA

    def far(x):
        return pltpu.with_memory_space_constraint(x, pltpu.HBM)

    def near(x):
        return pltpu.with_memory_space_constraint(x, pltpu.VMEM)

    gq, giw, kbuf, wbuf, table = pl.pallas_call(
        functools.partial(gather_kernel, n),
        out_shape=(
            pltpu.VMEM((n, rows, heads, PACKED), lq.dtype),
            pltpu.VMEM((n,) + iw.shape, iw.dtype),
            pltpu.VMEM(keys.shape, keys.dtype),
            pltpu.VMEM(weight.shape, weight.dtype),
            pltpu.VMEM((rows, HEAD_GROUPS, LANES), jnp.int32),
        ),
        in_specs=[hbm] * 6,
        out_specs=(vmem,) * 5,
        scratch_shapes=[
            pltpu.VMEM(lq.shape, lq.dtype),
            pltpu.VMEM(iq.shape, iq.dtype),
            pltpu.VMEM(sel.shape, sel.dtype),
            dma((6,)),
            dma((half, rows + 1)), dma((half, rows + 1)),
            dma((half, rows + 1)), dma((half, rows + 1)),
        ],
        compiler_params=pltpu.CompilerParams(
            collective_id=0, has_side_effects=True, vmem_limit_bytes=16 * MIB
        ),
        name="gather",
    )(far(lq), far(iq), far(iw), far(sel), far(keys), far(weight))

    pairs = rows * HEAD_GROUPS
    nsel = sel.shape[2]
    room = FIRST + -(-max(nsel - FIRST, 0) // MORE) * MORE
    own, sent, own_lse, sent_lse = pl.pallas_call(
        local_kernel,
        out_shape=(
            pltpu.VMEM((half, rows, heads, LATENT_WIDTH), jnp.float32),
            pltpu.VMEM((half, rows, heads, LATENT_WIDTH), jnp.bfloat16),
            pltpu.VMEM((half, heads, LANES), jnp.float32),
            pltpu.VMEM((half, heads, LANES), jnp.float32),
        ),
        in_specs=[smem, smem, vmem, hbm],
        out_specs=(vmem,) * 4,
        scratch_shapes=[
            pltpu.VMEM((pairs, width, room * LANES), cache.dtype),
            dma((pairs, nsel)),
        ],
        compiler_params=pltpu.CompilerParams(vmem_limit_bytes=44 * MIB),
        name="local",
    )(table, lengths, near(gq), far(jnp.swapaxes(cache, 1, 2)))

    steps = (half, rows + 1)
    attended, scores = pl.pallas_call(
        functools.partial(exchange_kernel, n),
        out_shape=(
            pltpu.VMEM((rows, heads, LATENT_WIDTH), jnp.bfloat16),
            pltpu.VMEM((rows, span), jnp.float32),
        ),
        in_specs=[smem] + [vmem] * 7,
        out_specs=(vmem, vmem),
        scratch_shapes=[
            pltpu.VMEM((rows, heads, LATENT_WIDTH), jnp.float32),
            pltpu.VMEM(sent.shape, sent.dtype),
            pltpu.VMEM(sent_lse.shape, sent_lse.dtype),
            pltpu.VMEM(sent.shape, sent.dtype),
            pltpu.VMEM(sent_lse.shape, sent_lse.dtype),
            pltpu.VMEM(sent.shape, sent.dtype),
            pltpu.VMEM(sent_lse.shape, sent_lse.dtype),
            dma(steps), dma(steps), dma(steps), dma(steps),
        ],
        compiler_params=pltpu.CompilerParams(
            collective_id=1, has_side_effects=True, vmem_limit_bytes=16 * MIB
        ),
        name="exchange",
    )(
        lengths, near(own), near(sent), near(own_lse), near(sent_lse),
        near(gq), near(giw), near(kbuf),
    )

    head_out, index_scores = pl.pallas_call(
        project_kernel,
        out_shape=(
            jax.ShapeDtypeStruct((rows, heads, weight.shape[2]), jnp.bfloat16),
            jax.ShapeDtypeStruct((rows, span), jnp.float32),
        ),
        in_specs=[vmem, vmem, vmem],
        out_specs=(vmem, hbm),
        scratch_shapes=[dma((1,))],
        compiler_params=pltpu.CompilerParams(vmem_limit_bytes=16 * MIB),
        name="project",
    )(near(attended), near(wbuf), near(scores))
    return (index_scores[None], head_out[None])


def solution(mesh):
    return jax.shard_map(
        functools.partial(on_device, mesh.shape["seq"]),
        mesh=mesh,
        in_specs=(
            P("section", "groups", "seq", None),
            P("section", "groups", "seq", None),
            P("section", "groups", "seq", None),
            P("section", "groups", "seq", None),
            P("section", "groups", "seq"),
            P("section", "seq", None, None),
            P("section", "groups", None, None),
            P("groups"),
        ),
        out_specs=(P("section", "groups", "seq"), P("section", "groups", "seq", None)),
        check_vma=False,
    )
```

time: 54.5 us -> 43.3 us (0.79)
  the two profiles are of different devices: /device:TPU:14 before, /device:TPU:0 now
where the time goes in v1:
time: 43.3 us; the launch traced here: 43.1 us
  Pallas kernels  42.4 us (98%)
  between operations  0.67 us (2%)
    pallas_call x1, Pallas kernels, on_device(): pl.pallas_call(functools.partial(gather_kernel, n), out_shape=(pltpu.VMEM...  17.9 us
    pallas_call x1, Pallas kernels, on_device(): pl.pallas_call(functools.partial(exchange_kernel, n), out_shape=(pltpu.VM...  12.2 us
    pallas_call x1, Pallas kernels, on_device(): pl.pallas_call(local_kernel, out_shape=(pltpu.VMEM((half, rows, heads, LA...  10.8 us
    pallas_call x1, Pallas kernels, on_device(): pl.pallas_call(project_kernel, out_shape=(jax.ShapeDtypeStruct((rows, hea...  1.56 us

profile of v1, /device:TPU:0, one launch (start us, length us, event | category | flops | bytes accessed | tf_op | source)
XLA Modules:
  0.0 43.1 jit_solution(1146976194415884741)
XLA Ops:
  0.6 0.0 copy-start
  0.6 17.9 %gather.1 = (bf16[8,4,16,640]{3,2,1,0:T(8,128)(2,1)S(1)}, bf16[8,4,8]{2,1,0:T(4,128)(2,1)S(1)}, bf16[4,4096,128]{2,1,0:T(8,128)(2,1)S(1)}, bf16[16,512,128]{2,1,0:T(8,128)(2,1)S(1)}, s32[4,2,128]{2,1,0:T(2,128)S(1)}) custom-call(bf16[4,16,576]{2,1,0:T(8,128)(2,1)} %bitcast.14, bf16[4,8,128]{2,1,0:T(8,128)(2,1)} %bitcast.15, bf16[4,8]{1,0:T(4,128)(2,1)} %bitcast.17, ...), custom_call_target="tpu_custom_call" | custom-call | tf_op jit(solution)/shard_map/gather/pallas_call | solution.py:456
  18.5 0.0 copy-done
  18.5 10.8 %local.1 = (f32[4,4,16,512]{3,2,1,0:T(8,128)S(1)}, bf16[4,4,16,512]{3,2,1,0:T(8,128)(2,1)S(1)}, f32[4,16,128]{2,1,0:T(8,128)S(1)}, f32[4,16,128]{2,1,0:T(8,128)S(1)}) custom-call(s32[4,2,128]{2,1,0:T(2,128)S(1)} %get-tuple-element.15.table, s32[4]{0:T(128)S(1)} %copy-done, bf16[8,4,16,640]{3,2,1,0:T(8,128)(2,1)S(1)} %get-tuple-element.16.gq, ...), custom_call_target="tpu_custom_call" | custom-call | tf_op jit(solution)/shard_map/local/pallas_call | solution.py:484
  29.3 12.2 %exchange.1 = (bf16[4,16,512]{2,1,0:T(8,128)(2,1)S(1)}, f32[4,4096]{1,0:T(4,128)S(1)}) custom-call(s32[4]{0:T(128)S(1)} %copy-done, f32[4,4,16,512]{3,2,1,0:T(8,128)S(1)} %get-tuple-element.17.own, bf16[4,4,16,512]{3,2,1,0:T(8,128)(2,1)S(1)} %get-tuple-element.18.sent, f32[4,16,128]{2,1,0:T(8,128)S(1)} %get-tuple-element.19.own_lse, ...), custom_call_target="tpu_custom_call" | custom-call | tf_op jit(solution)/shard_map/exchange/pallas_call | solution.py:503
  41.5 1.6 %project.1 = (bf16[4,16,128]{2,1,0:T(8,128)(2,1)}, f32[4,4096]{1,0:T(4,128)}) custom-call(bf16[4,16,512]{2,1,0:T(8,128)(2,1)S(1)} %get-tuple-element.23.attended, bf16[16,512,128]{2,1,0:T(8,128)(2,1)S(1)} %get-tuple-element.24.weight, f32[4,4096]{1,0:T(4,128)S(1)} %get-tuple-element.25.scores), custom_call_target="tpu_custom_call" | custom-call | tf_op jit(solution)/shard_map/project/pallas_call | solution.py:530
Async XLA Ops:
  0.6 17.9 %copy-start = (s32[4]{0:T(128)S(1)}, s32[4]{0:T(128)}, u32[]{:S(2)}) copy-start(s32[4]{0:T(128)} %lens.3) | copy-start | bytes 52

commit v2 on v1

--- a/solution.py
+++ b/solution.py
@@ -15,8 +15,9 @@
 HEAD_GROUPS = 2
 NEG = -1e30
 LOG2E = 1.4426950408889634
-FIRST = 8
-MORE = 4
+FIRST = 4
+MORE = 2
+STRIP = 256
 LANES = 128
 PACKED = LATENT_WIDTH + LANES
 MIB = 1024 * 1024
@@ -73,7 +74,7 @@
 
 
 def gather_kernel(
-    n, lq, iq, iw, sel, keys, weight, gq, giw, kbuf, wbuf, table,
+    n, lq, iq, iw, sel, cache, keys, weight, gq, giw, cbuf, kbuf, wbuf, table,
     lqs, iqs, sels, load_sem, zsend, zrecv, ysend, yrecv,
 ):
     line = Line(n)
@@ -89,7 +90,17 @@
         pltpu.make_async_copy(keys, kbuf, load_sem.at[4]),
         pltpu.make_async_copy(weight, wbuf, load_sem.at[5]),
     ]
-    for copy in loads:
+    strips = cbuf.shape[1]
+    for b in range(rows):
+        for j in range(strips):
+            loads.append(
+                pltpu.make_async_copy(
+                    cache.at[b, :, pl.ds(j * STRIP, STRIP)],
+                    cbuf.at[b, j],
+                    load_sem.at[6 + b * strips + j],
+                )
+            )
+    for copy in loads[:4] + loads[6:] + loads[4:6]:
         copy.start()
     for copy in loads[:3]:
         copy.wait()
@@ -132,21 +143,26 @@
     first = me * here
     chosen = sels[...]
     spots = lax.broadcasted_iota(jnp.int32, table.shape, 2)
-    kept = jnp.full(table.shape, -1, jnp.int32)
-    count = jnp.zeros(table.shape, jnp.int32)
+    kept = jnp.zeros(table.shape, jnp.int32)
+    counts = [jnp.zeros(table.shape, jnp.int32)] * 2
+    nsel = (LANES - 2) // 2
     for i in range(sels.shape[2]):
         block = jnp.broadcast_to(chosen[:, :, i : i + 1], table.shape)
         mine = (block >= first) & (block < first + here)
-        kept = jnp.where(mine & (spots == count), block, kept)
-        count = count + jnp.where(mine, 1, 0)
-    table[...] = jnp.where(spots == LANES - 1, count, kept)
+        odd = block & 1
+        for part in range(2):
+            take = mine & (odd == part)
+            kept = jnp.where(take & (spots == part * nsel + counts[part]), block, kept)
+            counts[part] = counts[part] + jnp.where(take, 1, 0)
+    kept = jnp.where(spots == LANES - 2, counts[0], kept)
+    table[...] = jnp.where(spots == LANES - 1, counts[1], kept)
 
     for r in range(rows, -1, -1):
         for k in line.order:
             along[k, r].wait_recv()
             onward[k, r].start()
-    loads[4].wait()
-    loads[5].wait()
+    for copy in loads[4:]:
+        copy.wait()
     for r in range(rows, -1, -1):
         across[r].wait_recv()
         for k in line.order:
@@ -158,45 +174,16 @@
             onward[k, r].wait_send()
 
 
-def local_kernel(table, lens, gq, cache, own, sent, own_lse, sent_lse, buf, sems):
+def local_kernel(table, lens, gq, cache, own, sent, own_lse, sent_lse):
     me = lax.axis_index("seq")
     side = lax.rem(me, 2)
-    rows, width, span = cache.shape
-    here = span // BLOCK
-    first = me * here
-    pairs = rows * HEAD_GROUPS
-
-    def count_of(b, g):
-        return table[b, g, LANES - 1]
-
-    def block_copy(b, g, block, slot):
-        rg = b * HEAD_GROUPS + g
-        start = pl.multiple_of((block - first) // 2 * LANES, LANES)
-        dest = pl.multiple_of(slot * LANES, LANES)
-        return pltpu.make_async_copy(
-            cache.at[b, :, pl.ds(start, LANES)],
-            buf.at[rg, :, pl.ds(dest, LANES)],
-            sems.at[rg, slot],
-        )
-
-    @pl.loop(0, pairs)
-    def _(rg):
-        b, g = rg // HEAD_GROUPS, rg % HEAD_GROUPS
-
-        @pl.loop(0, count_of(b, g))
-        def _(slot):
-            block_copy(b, g, table[b, g, slot], slot).start()
-
-    @pl.loop(0, pairs)
-    def _(rg):
-        count = count_of(rg // HEAD_GROUPS, rg % HEAD_GROUPS)
-        extra = jnp.maximum(count - FIRST, 0)
-        room = FIRST + (extra + MORE - 1) // MORE * MORE
-
-        @pl.loop(count, room)
-        def _(slot):
-            dest = pl.multiple_of(slot * LANES, LANES)
-            buf[rg, :, pl.ds(dest, LANES)] = jnp.zeros((width, LANES), jnp.bfloat16)
+    rows, strips, width, _ = cache.shape
+    first = me * (strips * STRIP // BLOCK)
+    per_strip = STRIP // LANES
+    nsel = (LANES - 2) // 2
+
+    def count_of(b, g, part):
+        return table[b, g, LANES - 2 + part]
 
     heads = gq.shape[2]
     per_group = gq.shape[0] // HEAD_GROUPS
@@ -205,41 +192,38 @@
     lane = lax.broadcasted_iota(jnp.int32, (1, LANES), 1)
     spot = lax.broadcasted_iota(jnp.int32, (per_group // 2, heads, LANES), 2)
 
-    def scores(b, g, query, base, slots):
-        rg = b * HEAD_GROUPS + g
-        count = count_of(b, g)
-        bias = []
-        for j in range(slots):
-            slot = base + j
-            block = table[b, g, slot]
-            begin = block % 2 * BLOCK
+    def latents(b, g, j):
+        tiles, ends = [], []
+        for part in range(2):
+            held = j < count_of(b, g, part)
+            block = table[b, g, part * nsel + j]
+            tile = jnp.where(held, (block - first) // 2, 0)
+            start = pl.multiple_of(tile % per_strip * LANES, LANES)
+            tiles.append(cache[b, tile // per_strip, :, pl.ds(start, LANES)])
             live = jnp.minimum(BLOCK, lens[b] - block * BLOCK)
-            end = jnp.where(slot < count, begin + live, 0)
-            bias.append(jnp.where((lane >= begin) & (lane < end), 0.0, NEG))
-        bias = jnp.concatenate(bias, axis=1)
-        start = base * LANES
-        if not isinstance(start, int):
-            start = pl.multiple_of(start, MORE * LANES)
-        window = pl.ds(start, slots * LANES)
-        s = jnp.dot(query, buf[rg, :, window], preferred_element_type=jnp.float32)
-        return s * scale + bias, window
-
-    def mix(b, g, p, window):
+            ends.append(part * BLOCK + jnp.where(held, live, 0))
+        usable = (lane < ends[0]) | ((lane >= BLOCK) & (lane < ends[1]))
+        low, high = tiles
+        both = jnp.concatenate([low[:, :BLOCK], high[:, BLOCK:]], axis=1)
+        return both, jnp.where(usable, 0.0, NEG)
+
+    def chunk(b, g, query, base, tiles):
+        parts = [latents(b, g, base + j) for j in range(tiles)]
+        keys = jnp.concatenate([part for part, _ in parts], axis=1)
+        bias = jnp.concatenate([part for _, part in parts], axis=1)
+        s = jnp.dot(query, keys, preferred_element_type=jnp.float32)
+        return s * scale + bias, keys
+
+    def mix(p, keys):
         return lax.dot_general(
             p.astype(jnp.bfloat16),
-            buf[b * HEAD_GROUPS + g, :LATENT_WIDTH, window],
+            keys[:LATENT_WIDTH],
             (((1,), (1,)), ((), ())),
             preferred_element_type=jnp.float32,
         )
 
     @pl.loop(0, rows)
     def _(b):
-        for g in range(HEAD_GROUPS):
-
-            @pl.loop(0, count_of(b, g))
-            def _(slot, g=g):
-                block_copy(b, g, first, slot).wait()
-
         queries, state = [], []
         for g in range(HEAD_GROUPS):
             query = gq[pl.ds(g * per_group, per_group), b]
@@ -247,29 +231,28 @@
                 query = query.astype(jnp.float32)
             query = query.reshape(wide, PACKED)[:, :width].astype(jnp.bfloat16)
             queries.append(query)
-        firsts = [scores(b, g, queries[g], 0, FIRST) for g in range(HEAD_GROUPS)]
-        for g, (s, window) in enumerate(firsts):
+        firsts = [chunk(b, g, queries[g], 0, FIRST) for g in range(HEAD_GROUPS)]
+        for g, (s, keys) in enumerate(firsts):
             top = jnp.max(s, axis=1, keepdims=True)
             p = jnp.exp2(s - top)
-            state.append((top, jnp.sum(p, axis=1, keepdims=True), mix(b, g, p, window)))
+            state.append((top, jnp.sum(p, axis=1, keepdims=True), mix(p, keys)))
 
         for g in range(HEAD_GROUPS):
 
             def more(c, carry, g=g):
                 top, total, acc = carry
-                s, window = scores(b, g, queries[g], FIRST + c * MORE, MORE)
+                s, keys = chunk(b, g, queries[g], FIRST + c * MORE, MORE)
                 new = jnp.maximum(top, jnp.max(s, axis=1, keepdims=True))
                 p = jnp.exp2(s - new)
                 keep = jnp.exp2(top - new)
                 total = total * keep + jnp.sum(p, axis=1, keepdims=True)
-                return new, total, acc * keep + mix(b, g, p, window)
-
-            extra = jnp.maximum(count_of(b, g) - FIRST, 0)
-            top, total, acc = lax.fori_loop(0, (extra + MORE - 1) // MORE, more, state[g])
-            acc = (acc / total).reshape(per_group, heads, LATENT_WIDTH)
+                return new, total, acc * keep + mix(p, keys)
+
+            extra = jnp.maximum(count_of(b, g, 0), count_of(b, g, 1)) - FIRST
+            steps = (jnp.maximum(extra, 0) + MORE - 1) // MORE
+            top, total, acc = lax.fori_loop(0, steps, more, state[g])
+            acc = (acc * (1.0 / total)).reshape(per_group // 2, 2, heads, LATENT_WIDTH)
             lse = jnp.broadcast_to(top + jnp.log2(total), (wide, LANES))
-            lse = lse.reshape(per_group, heads, LANES)
-            acc = acc.reshape(per_group // 2, 2, heads, LATENT_WIDTH)
             lse = lse.reshape(per_group // 2, 2, heads, LANES)
             here_z = pl.ds(g * per_group // 2, per_group // 2)
             even = side == 0
@@ -453,22 +436,23 @@
     def near(x):
         return pltpu.with_memory_space_constraint(x, pltpu.VMEM)
 
-    gq, giw, kbuf, wbuf, table = pl.pallas_call(
+    gq, giw, cbuf, kbuf, wbuf, table = pl.pallas_call(
         functools.partial(gather_kernel, n),
         out_shape=(
             pltpu.VMEM((n, rows, heads, PACKED), lq.dtype),
             pltpu.VMEM((n,) + iw.shape, iw.dtype),
+            pltpu.VMEM((rows, span // STRIP, width, STRIP), cache.dtype),
             pltpu.VMEM(keys.shape, keys.dtype),
             pltpu.VMEM(weight.shape, weight.dtype),
             pltpu.VMEM((rows, HEAD_GROUPS, LANES), jnp.int32),
         ),
-        in_specs=[hbm] * 6,
-        out_specs=(vmem,) * 5,
+        in_specs=[hbm] * 7,
+        out_specs=(vmem,) * 6,
         scratch_shapes=[
             pltpu.VMEM(lq.shape, lq.dtype),
             pltpu.VMEM(iq.shape, iq.dtype),
             pltpu.VMEM(sel.shape, sel.dtype),
-            dma((6,)),
+            dma((6 + rows * (span // STRIP),)),
             dma((half, rows + 1)), dma((half, rows + 1)),
             dma((half, rows + 1)), dma((half, rows + 1)),
         ],
@@ -476,11 +460,11 @@
             collective_id=0, has_side_effects=True, vmem_limit_bytes=16 * MIB
         ),
         name="gather",
-    )(far(lq), far(iq), far(iw), far(sel), far(keys), far(weight))
-
-    pairs = rows * HEAD_GROUPS
-    nsel = sel.shape[2]
-    room = FIRST + -(-max(nsel - FIRST, 0) // MORE) * MORE
+    )(
+        far(lq), far(iq), far(iw), far(sel), far(jnp.swapaxes(cache, 1, 2)),
+        far(keys), far(weight),
+    )
+
     own, sent, own_lse, sent_lse = pl.pallas_call(
         local_kernel,
         out_shape=(
@@ -489,15 +473,11 @@
             pltpu.VMEM((half, heads, LANES), jnp.float32),
             pltpu.VMEM((half, heads, LANES), jnp.float32),
         ),
-        in_specs=[smem, smem, vmem, hbm],
+        in_specs=[smem, smem, vmem, vmem],
         out_specs=(vmem,) * 4,
-        scratch_shapes=[
-            pltpu.VMEM((pairs, width, room * LANES), cache.dtype),
-            dma((pairs, nsel)),
-        ],
-        compiler_params=pltpu.CompilerParams(vmem_limit_bytes=44 * MIB),
+        compiler_params=pltpu.CompilerParams(vmem_limit_bytes=16 * MIB),
         name="local",
-    )(table, lengths, near(gq), far(jnp.swapaxes(cache, 1, 2)))
+    )(table, lengths, near(gq), near(cbuf))
 
     steps = (half, rows + 1)
     attended, scores = pl.pallas_call(

time: 43.3 us -> 39.1 us (0.903); the launches traced: 43.1 us -> 39.5 us
  Pallas kernels: 42.4 us -> 38.8 us
    pallas_call x1, Pallas kernels: 10.8 us -> 6.56 us  [on_device(): pl.pallas_call(local_kernel, out_shape=(pltpu.VMEM((half, rows, heads, LA...]
    pallas_call x1, Pallas kernels: 17.9 us -> 18.4 us  [on_device(): pl.pallas_call(functools.partial(gather_kernel, n), out_shape=(pltpu.VMEM...]
where the time goes in v2:
time: 39.1 us; the launch traced here: 39.5 us
  Pallas kernels  38.8 us (99%)
  between operations  0.67 us (2%)
    pallas_call x1, Pallas kernels, on_device(): pl.pallas_call(functools.partial(gather_kernel, n), out_shape=(pltpu.VMEM...  18.4 us
    pallas_call x1, Pallas kernels, on_device(): pl.pallas_call(functools.partial(exchange_kernel, n), out_shape=(pltpu.VM...  12.3 us
    pallas_call x1, Pallas kernels, on_device(): pl.pallas_call(local_kernel, out_shape=(pltpu.VMEM((half, rows, heads, LA...  6.56 us
    pallas_call x1, Pallas kernels, on_device(): pl.pallas_call(project_kernel, out_shape=(jax.ShapeDtypeStruct((rows, hea...  1.55 us

profile of v2, /device:TPU:0, one launch (start us, length us, event | category | flops | bytes accessed | tf_op | source)
XLA Modules:
  0.0 39.5 jit_solution(1395979807352069371)
XLA Ops:
  0.6 0.0 copy-start
  0.6 18.4 %gather.1 = (bf16[8,4,16,640]{3,2,1,0:T(8,128)(2,1)S(1)}, bf16[8,4,8]{2,1,0:T(4,128)(2,1)S(1)}, bf16[4,16,576,256]{3,2,1,0:T(8,128)(2,1)S(1)}, bf16[4,4096,128]{...) custom-call(bf16[4,16,576]{2,1,0:T(8,128)(2,1)} %bitcast.14, ...), custom_call_target="tpu_custom_call" | custom-call | tf_op jit(solution)/shard_map/gather/pallas_call | solution.py:439
  19.1 0.0 copy-done
  19.1 6.6 %local.1 = (f32[4,4,16,512]{3,2,1,0:T(8,128)S(1)}, bf16[4,4,16,512]{3,2,1,0:T(8,128)(2,1)S(1)}, f32[4,16,128]{2,1,0:T(8,128)S(1)}, f32[4,16,128]{2,1,0:T(8,128)S(1)}) custom-call(s32[4,2,128]{2,1,0:T(2,128)S(1)} %get-tuple-element.16.table, s32[4]{0:T(128)S(1)} %copy-done, bf16[8,4,16,640]{3,2,1,0:T(8,128)(2,1)S(1)} %get-tuple-element.17.gq, ...), custom_call_target="tpu_custom_call" | custom-call | tf_op jit(solution)/shard_map/local/pallas_call | solution.py:468
  25.6 12.3 %exchange.1 = (bf16[4,16,512]{2,1,0:T(8,128)(2,1)S(1)}, f32[4,4096]{1,0:T(4,128)S(1)}) custom-call(s32[4]{0:T(128)S(1)} %copy-done, f32[4,4,16,512]{3,2,1,0:T(8,128)S(1)} %get-tuple-element.19.own, bf16[4,4,16,512]{3,2,1,0:T(8,128)(2,1)S(1)} %get-tuple-element.20.sent, f32[4,16,128]{2,1,0:T(8,128)S(1)} %get-tuple-element.21.own_lse, ...), custom_call_target="tpu_custom_call" | custom-call | tf_op jit(solution)/shard_map/exchange/pallas_call | solution.py:483
  37.9 1.6 %project.1 = (bf16[4,16,128]{2,1,0:T(8,128)(2,1)}, f32[4,4096]{1,0:T(4,128)}) custom-call(bf16[4,16,512]{2,1,0:T(8,128)(2,1)S(1)} %get-tuple-element.25.attended, bf16[16,512,128]{2,1,0:T(8,128)(2,1)S(1)} %get-tuple-element.26.weight, f32[4,4096]{1,0:T(4,128)S(1)} %get-tuple-element.27.scores), custom_call_target="tpu_custom_call" | custom-call | tf_op jit(solution)/shard_map/project/pallas_call | solution.py:510
Async XLA Ops:
  0.6 18.4 %copy-start = (s32[4]{0:T(128)S(1)}, s32[4]{0:T(128)}, u32[]{:S(2)}) copy-start(s32[4]{0:T(128)} %lens.3) | copy-start | bytes 52

commit v3 on v2

--- a/solution.py
+++ b/solution.py
@@ -52,14 +52,18 @@
     def device(self, z):
         return 2 * z + self.y
 
+    def opposite(self, z):
+        return 2 * z + 1 - self.y
+
     def greet(self):
         barrier = pltpu.get_barrier_semaphore()
-        peers = [self.partner] + [self.device(self.to(k)) for k in self.order]
-        for peer in peers:
+        n = 2 * self.half
+        for k in range(1, n):
+            peer = lax.rem(self.me + k, n)
             pl.semaphore_signal(
                 barrier, inc=1, device_id={"seq": peer}, device_id_type=MESH
             )
-        return lambda: pl.semaphore_wait(barrier, self.half)
+        return lambda: pl.semaphore_wait(barrier, n - 1)
 
 
 def push(peer, src, dst, send_sem, recv_sem):
@@ -75,7 +79,7 @@
 
 def gather_kernel(
     n, lq, iq, iw, sel, cache, keys, weight, gq, giw, cbuf, kbuf, wbuf, table,
-    lqs, iqs, sels, load_sem, zsend, zrecv, ysend, yrecv,
+    lqs, iqs, sels, load_sem, zsend, zrecv, ysend, yrecv, dsend, drecv,
 ):
     line = Line(n)
     me = line.me
@@ -123,7 +127,7 @@
     def pieces(owner):
         return [gq.at[owner, b] for b in range(rows)] + [giw.at[owner]]
 
-    across, along, onward = [], {}, {}
+    across, along, onward, slant = [], {}, {}, {}
     for r, ref in enumerate(pieces(me)):
         across.append(push(line.partner, ref, ref, ysend.at[0, r], yrecv.at[0, r]))
         for k in line.order:
@@ -131,11 +135,17 @@
                 line.device(line.to(k)), ref, ref, zsend.at[k, r], zrecv.at[k, r]
             )
     for k in line.order:
+        ref = pieces(me)[0]
+        slant[k] = push(line.opposite(line.to(k)), ref, ref, dsend.at[k], drecv.at[k])
         for r, ref in enumerate(pieces(line.device(line.frm(k)))):
+            if r == 0:
+                continue
             onward[k, r] = push(line.partner, ref, ref, ysend.at[k, r], yrecv.at[k, r])
     for r in range(rows, -1, -1):
         for k in line.order:
             along[k, r].start()
+            if r == 0:
+                slant[k].start()
         across[r].start()
 
     loads[3].wait()
@@ -157,24 +167,20 @@
     kept = jnp.where(spots == LANES - 2, counts[0], kept)
     table[...] = jnp.where(spots == LANES - 1, counts[1], kept)
 
-    for r in range(rows, -1, -1):
+    for r in range(rows, 0, -1):
         for k in line.order:
             along[k, r].wait_recv()
             onward[k, r].start()
     for copy in loads[4:]:
         copy.wait()
-    for r in range(rows, -1, -1):
-        across[r].wait_recv()
-        for k in line.order:
-            onward[k, r].wait_recv()
-    for r in range(rows, -1, -1):
-        across[r].wait_send()
-        for k in line.order:
-            along[k, r].wait_send()
-            onward[k, r].wait_send()
-
-
-def local_kernel(table, lens, gq, cache, own, sent, own_lse, sent_lse):
+    direct = [along[k, 0] for k in line.order] + list(slant.values())
+    for copy in direct + across + list(onward.values()):
+        copy.wait_recv()
+    for copy in across + list(along.values()) + list(onward.values()) + list(slant.values()):
+        copy.wait_send()
+
+
+def local_kernel(table, lens, gq, cache, own, own_first, sent, lse_out):
     me = lax.axis_index("seq")
     side = lax.rem(me, 2)
     rows, strips, width, _ = cache.shape
@@ -190,7 +196,8 @@
     wide = per_group * heads
     scale = (VALUE_WIDTH + ROTARY_WIDTH) ** (-0.5) * LOG2E
     lane = lax.broadcasted_iota(jnp.int32, (1, LANES), 1)
-    spot = lax.broadcasted_iota(jnp.int32, (per_group // 2, heads, LANES), 2)
+    head = lax.broadcasted_iota(jnp.int32, (wide, LANES), 0)
+    spot = lax.broadcasted_iota(jnp.int32, (wide, LANES), 1)
 
     def latents(b, g, j):
         tiles, ends = [], []
@@ -237,39 +244,48 @@
             p = jnp.exp2(s - top)
             state.append((top, jnp.sum(p, axis=1, keepdims=True), mix(p, keys)))
 
-        for g in range(HEAD_GROUPS):
-
-            def more(c, carry, g=g):
-                top, total, acc = carry
-                s, keys = chunk(b, g, queries[g], FIRST + c * MORE, MORE)
+        def more(c, carry):
+            after = []
+            chunks = [
+                chunk(b, g, queries[g], FIRST + c * MORE, MORE) for g in range(HEAD_GROUPS)
+            ]
+            for (s, keys), (top, total, acc) in zip(chunks, carry):
                 new = jnp.maximum(top, jnp.max(s, axis=1, keepdims=True))
                 p = jnp.exp2(s - new)
                 keep = jnp.exp2(top - new)
                 total = total * keep + jnp.sum(p, axis=1, keepdims=True)
-                return new, total, acc * keep + mix(p, keys)
-
-            extra = jnp.maximum(count_of(b, g, 0), count_of(b, g, 1)) - FIRST
-            steps = (jnp.maximum(extra, 0) + MORE - 1) // MORE
-            top, total, acc = lax.fori_loop(0, steps, more, state[g])
+                after.append((new, total, acc * keep + mix(p, keys)))
+            return after
+
+        extra = functools.reduce(
+            jnp.maximum,
+            [count_of(b, g, part) for g in range(HEAD_GROUPS) for part in range(2)],
+        )
+        extra = jnp.maximum(extra - FIRST, 0)
+        state = lax.fori_loop(0, (extra + MORE - 1) // MORE, more, state)
+        lses = jnp.zeros((1, LANES), jnp.float32)
+        for g, (top, total, acc) in enumerate(state):
             acc = (acc * (1.0 / total)).reshape(per_group // 2, 2, heads, LATENT_WIDTH)
             lse = jnp.broadcast_to(top + jnp.log2(total), (wide, LANES))
-            lse = lse.reshape(per_group // 2, 2, heads, LANES)
+            lse = jnp.where(spot == head + g * wide, lse, 0.0)
+            lses += jnp.sum(lse, axis=0, keepdims=True)
             here_z = pl.ds(g * per_group // 2, per_group // 2)
             even = side == 0
-            own[here_z, b] = jnp.where(even, acc[:, 0], acc[:, 1])
+            mine = jnp.where(even, acc[:, 0], acc[:, 1])
+            own[here_z, b] = mine
             sent[here_z, b] = jnp.where(even, acc[:, 1], acc[:, 0]).astype(jnp.bfloat16)
-            own_lse[here_z] = jnp.where(
-                spot == b, jnp.where(even, lse[:, 0], lse[:, 1]), own_lse[here_z]
-            )
-            sent_lse[here_z] = jnp.where(
-                spot == b, jnp.where(even, lse[:, 1], lse[:, 0]), sent_lse[here_z]
-            )
+
+            @pl.when(b == 0)
+            def _(mine=mine, here_z=here_z):
+                own_first[here_z] = mine.astype(jnp.bfloat16)
+
+        lse_out[pl.ds(b, 1)] = lses
 
 
 def exchange_kernel(
-    n, lens, own, sent, own_lse, sent_lse, gq, giw, kbuf, attended, scores,
-    kept, from_pair, pair_lse, joint, joint_lse, from_line, line_lse,
-    ysend, yrecv, zsend, zrecv,
+    n, lens, own, own_first, sent, lse, gq, giw, kbuf, attended, scores,
+    kept, from_pair, joint, from_line, firsts, lses, share, share_first,
+    ysend, yrecv, zsend, zrecv, fsend, frecv, lsend, lrecv,
 ):
     line = Line(n)
     half, me = line.half, line.me
@@ -278,14 +294,27 @@
     entered()
 
     ring = line.order + [0]
-    across, along = {}, {}
+    across, along, first, told = {}, {}, {}, {}
+    for k in range(1, n):
+        told[k] = push(
+            lax.rem(me + k, n), lse, lses.at[me], lsend.at[k], lrecv.at[k]
+        )
+        told[k].start()
     for k in ring:
         z = line.to(k)
-        refs = [(sent_lse.at[z], pair_lse.at[z])]
-        refs += [(sent.at[z, b], from_pair.at[z, b]) for b in range(rows)]
-        for r, (src, dst) in enumerate(refs):
-            across[k, r] = push(line.partner, src, dst, ysend.at[k, r], yrecv.at[k, r])
-            across[k, r].start()
+        for b in range(1, rows):
+            across[k, b] = push(
+                line.partner, sent.at[z, b], from_pair.at[z, b], ysend.at[k, b], yrecv.at[k, b]
+            )
+            across[k, b].start()
+        peers = [(1, line.opposite(z), sent.at[z, 0])]
+        if k:
+            peers.append((0, line.device(z), own_first.at[z]))
+        for side, peer, src in peers:
+            first[k, side] = push(
+                peer, src, firsts.at[me], fsend.at[k, side], frecv.at[k, side]
+            )
+            first[k, side].start()
 
     span = kbuf.shape[1]
     tile = min(512, span)
@@ -333,59 +362,63 @@
 
         lax.fori_loop(0, span // tile, step, 0)
 
-    def weigh(parts):
-        best = functools.reduce(jnp.maximum, parts)
-        grown = [jnp.exp2(part - best) for part in parts]
-        whole = functools.reduce(jnp.add, grown)
-        return [part / whole for part in grown], best + jnp.log2(whole)
-
     early = rows // 2
     for b in range(early):
         index_row(b)
 
+    for copy in told.values():
+        copy.wait_recv()
+    lses[me] = lse[...]
+    table = [lses[s] for s in range(n)]
+    best = functools.reduce(jnp.maximum, table)
+    whole = functools.reduce(jnp.add, [jnp.exp2(part - best) for part in table])
+    best = best + jnp.log2(whole)
+    both = [jnp.exp2(lse[...] - best), jnp.exp2(lses[line.partner] - best)]
+    share[...] = jnp.transpose(jnp.concatenate(both, axis=0))
+    share_first[...] = jnp.transpose(
+        jnp.concatenate([jnp.exp2(part[0:1] - best[0:1]) for part in table], axis=0)
+    )
+
     for k in ring:
         z = line.to(k)
-        across[k, 0].wait_recv()
-        (mine, theirs), lse = weigh([own_lse[z], pair_lse[z]])
-        if k:
-            joint_lse[z] = lse
-            target = line.device(z)
-            along[k, 0] = push(
-                target, joint_lse.at[z], line_lse.at[line.z], zsend.at[k, 0], zrecv.at[k, 0]
-            )
-        else:
-            line_lse[z] = lse
-        for b in range(rows):
-            across[k, b + 1].wait_recv()
-            value = mine[:, b : b + 1] * own[z, b]
-            value += theirs[:, b : b + 1] * from_pair[z, b].astype(jnp.float32)
+        target = line.device(z)
+        part = share[pl.ds(pl.multiple_of(target * heads, heads), heads)]
+        for b in range(1, rows):
+            across[k, b].wait_recv()
+            value = part[:, b : b + 1] * own[z, b]
+            value += part[:, rows + b : rows + b + 1] * from_pair[z, b].astype(jnp.float32)
             if k:
                 joint[z, b] = value.astype(jnp.bfloat16)
-                along[k, b + 1] = push(
+                along[k, b] = push(
                     target, joint.at[z, b], from_line.at[line.z, b],
-                    zsend.at[k, b + 1], zrecv.at[k, b + 1],
+                    zsend.at[k, b], zrecv.at[k, b],
                 )
             else:
                 kept[b] = value
         if k:
-            for r in range(rows + 1):
-                along[k, r].start()
+            for b in range(1, rows):
+                along[k, b].start()
 
     for b in range(early, rows):
         index_row(b)
 
-    for k in line.order:
-        along[k, 0].wait_recv()
-    spans = [line.z] + [line.frm(k) for k in line.order]
-    factors, _ = weigh([line_lse[z] for z in spans])
-    for b in range(rows):
+    for copy in first.values():
+        copy.wait_recv()
+    firsts[me] = jnp.zeros((heads, latent), firsts.dtype)
+    part = share_first[pl.ds(pl.multiple_of(me * heads, heads), heads)]
+    mine = share[pl.ds(pl.multiple_of(me * heads, heads), heads)]
+    value = mine[:, 0:1] * own[line.z, 0]
+    for s in range(n):
+        value += part[:, s : s + 1] * firsts[s].astype(jnp.float32)
+    attended[0] = value.astype(attended.dtype)
+    for b in range(1, rows):
+        value = kept[b]
         for k in line.order:
-            along[k, b + 1].wait_recv()
-        value = factors[0][:, b : b + 1] * kept[b]
-        for z, factor in zip(spans[1:], factors[1:]):
-            value += factor[:, b : b + 1] * from_line[z, b].astype(jnp.float32)
+            along[k, b].wait_recv()
+            value += from_line[line.frm(k), b].astype(jnp.float32)
         attended[b] = value.astype(attended.dtype)
-    for copy in list(across.values()) + list(along.values()):
+    copies = [across, along, first, told]
+    for copy in [copy for group in copies for copy in group.values()]:
         copy.wait_send()
 
 
@@ -455,6 +488,7 @@
             dma((6 + rows * (span // STRIP),)),
             dma((half, rows + 1)), dma((half, rows + 1)),
             dma((half, rows + 1)), dma((half, rows + 1)),
+            dma((half,)), dma((half,)),
         ],
         compiler_params=pltpu.CompilerParams(
             collective_id=0, has_side_effects=True, vmem_limit_bytes=16 * MIB
@@ -465,13 +499,13 @@
         far(keys), far(weight),
     )
 
-    own, sent, own_lse, sent_lse = pl.pallas_call(
+    own, own_first, sent, lse = pl.pallas_call(
         local_kernel,
         out_shape=(
             pltpu.VMEM((half, rows, heads, LATENT_WIDTH), jnp.float32),
+            pltpu.VMEM((half, heads, LATENT_WIDTH), jnp.bfloat16),
             pltpu.VMEM((half, rows, heads, LATENT_WIDTH), jnp.bfloat16),
-            pltpu.VMEM((half, heads, LANES), jnp.float32),
-            pltpu.VMEM((half, heads, LANES), jnp.float32),
+            pltpu.VMEM((rows, n * heads), jnp.float32),
         ),
         in_specs=[smem, smem, vmem, vmem],
         out_specs=(vmem,) * 4,
@@ -479,7 +513,6 @@
         name="local",
     )(table, lengths, near(gq), near(cbuf))
 
-    steps = (half, rows + 1)
     attended, scores = pl.pallas_call(
         functools.partial(exchange_kernel, n),
         out_shape=(
@@ -491,19 +524,21 @@
         scratch_shapes=[
             pltpu.VMEM((rows, heads, LATENT_WIDTH), jnp.float32),
             pltpu.VMEM(sent.shape, sent.dtype),
-            pltpu.VMEM(sent_lse.shape, sent_lse.dtype),
             pltpu.VMEM(sent.shape, sent.dtype),
-            pltpu.VMEM(sent_lse.shape, sent_lse.dtype),
             pltpu.VMEM(sent.shape, sent.dtype),
-            pltpu.VMEM(sent_lse.shape, sent_lse.dtype),
-            dma(steps), dma(steps), dma(steps), dma(steps),
+            pltpu.VMEM((n, heads, LATENT_WIDTH), sent.dtype),
+            pltpu.VMEM((n,) + lse.shape, lse.dtype),
+            pltpu.VMEM((n * heads, 2 * rows), jnp.float32),
+            pltpu.VMEM((n * heads, n), jnp.float32),
+            dma((half, rows)), dma((half, rows)), dma((half, rows)), dma((half, rows)),
+            dma((half, 2)), dma((half, 2)), dma((n,)), dma((n,)),
         ],
         compiler_params=pltpu.CompilerParams(
             collective_id=1, has_side_effects=True, vmem_limit_bytes=16 * MIB
         ),
         name="exchange",
     )(
-        lengths, near(own), near(sent), near(own_lse), near(sent_lse),
+        lengths, near(own), near(own_first), near(sent), near(lse),
         near(gq), near(giw), near(kbuf),
     )
 

time: 39.1 us -> 40.2 us (1.028)
  Pallas kernels: 38.8 us -> 39.6 us
    pallas_call x1, Pallas kernels: 12.3 us -> 14.9 us  [on_device(): pl.pallas_call(functools.partial(exchange_kernel, n), out_shape=(pltpu.VM...]
    pallas_call x1, Pallas kernels: 6.56 us -> 4.39 us  [on_device(): pl.pallas_call(local_kernel, out_shape=(pltpu.VMEM((half, rows, heads, LA...]
where the time goes in v3:
time: 40.2 us; the launch traced here: 40.3 us
  Pallas kernels  39.6 us (99%)
  between operations  0.67 us (2%)
    pallas_call x1, Pallas kernels, on_device(): pl.pallas_call(functools.partial(gather_kernel, n), out_shape=(pltpu.VMEM...  18.8 us
    pallas_call x1, Pallas kernels, on_device(): pl.pallas_call(functools.partial(exchange_kernel, n), out_shape=(pltpu.VM...  14.9 us
    pallas_call x1, Pallas kernels, on_device(): pl.pallas_call(local_kernel, out_shape=(pltpu.VMEM((half, rows, heads, LA...  4.39 us
    pallas_call x1, Pallas kernels, on_device(): pl.pallas_call(project_kernel, out_shape=(jax.ShapeDtypeStruct((rows, hea...  1.55 us

profile of v3, /device:TPU:0, one launch (start us, length us, event | category | flops | bytes accessed | tf_op | source)
XLA Modules:
  0.0 40.3 jit_solution(8218460839343737509)
XLA Ops:
  0.6 0.0 copy-start
  0.6 18.8 %gather.1 = (bf16[8,4,16,640]{3,2,1,0:T(8,128)(2,1)S(1)}, bf16[8,4,8]{2,1,0:T(4,128)(2,1)S(1)}, bf16[4,16,576,256]{3,2,1,0:T(8,128)(2,1)S(1)}, bf16[4,4096,128]{...) custom-call(bf16[4,16,576]{2,1,0:T(8,128)(2,1)} %bitcast.14, ...), custom_call_target="tpu_custom_call" | custom-call | tf_op jit(solution)/shard_map/gather/pallas_call | solution.py:472
  19.4 0.0 copy-done
  19.4 4.4 %local.1 = (f32[4,4,16,512]{3,2,1,0:T(8,128)S(1)}, bf16[4,16,512]{2,1,0:T(8,128)(2,1)S(1)}, bf16[4,4,16,512]{3,2,1,0:T(8,128)(2,1)S(1)}, f32[4,128]{1,0:T(4,128)S(1)}) custom-call(s32[4,2,128]{2,1,0:T(2,128)S(1)} %get-tuple-element.16.table, s32[4]{0:T(128)S(1)} %copy-done, bf16[8,4,16,640]{3,2,1,0:T(8,128)(2,1)S(1)} %get-tuple-element.17.gq, ...), custom_call_target="tpu_custom_call" | custom-call | tf_op jit(solution)/shard_map/local/pallas_call | solution.py:502
  23.9 14.9 %exchange.1 = (bf16[4,16,512]{2,1,0:T(8,128)(2,1)S(1)}, f32[4,4096]{1,0:T(4,128)S(1)}) custom-call(s32[4]{0:T(128)S(1)} %copy-done, f32[4,4,16,512]{3,2,1,0:T(8,128)S(1)} %get-tuple-element.19.own, bf16[4,16,512]{2,1,0:T(8,128)(2,1)S(1)} %get-tuple-element.20.own_first, bf16[4,4,16,512]{3,2,1,0:T(8,128)(2,1)S(1)} %get-tuple-element.21.sent, ...), custom_call_target="tpu_custom_call" | custom-call | tf_op jit(solution)/shard_map/exchange/pallas_call | solution.py:516
  38.8 1.6 %project.1 = (bf16[4,16,128]{2,1,0:T(8,128)(2,1)}, f32[4,4096]{1,0:T(4,128)}) custom-call(bf16[4,16,512]{2,1,0:T(8,128)(2,1)S(1)} %get-tuple-element.25.attended, bf16[16,512,128]{2,1,0:T(8,128)(2,1)S(1)} %get-tuple-element.26.weight, f32[4,4096]{1,0:T(4,128)S(1)} %get-tuple-element.27.scores), custom_call_target="tpu_custom_call" | custom-call | tf_op jit(solution)/shard_map/project/pallas_call | solution.py:545
Async XLA Ops:
  0.6 18.8 %copy-start = (s32[4]{0:T(128)S(1)}, s32[4]{0:T(128)}, u32[]{:S(2)}) copy-start(s32[4]{0:T(128)} %lens.3) | copy-start | bytes 52

commit v4 on v2

v4 whole, which is shorter than its diff:
```python
import functools

import jax
import jax.numpy as jnp
from jax import lax
from jax.experimental import pallas as pl
from jax.experimental.pallas import tpu as pltpu
from jax.sharding import PartitionSpec as P

LATENT_WIDTH = 512
ROTARY_WIDTH = 64
VALUE_WIDTH = 128
IDX_DIM = 128
BLOCK = 64
HEAD_GROUPS = 2
NEG = -1e30
LOG2E = 1.4426950408889634
FIRST = 4
MORE = 2
STRIP = 128
EARLY = 2
SLOTS = 62
LANES = 128
PACKED = LATENT_WIDTH + LANES
MIB = 1024 * 1024
MESH = pl.DeviceIdType.MESH


class Line:
    def __init__(self, n):
        self.half = n // 2
        self.me = lax.axis_index("seq")
        self.z = lax.div(self.me, 2)
        self.y = lax.rem(self.me, 2)
        self.partner = self.me + 1 - 2 * self.y
        self.order = list(range(1, self.half))
        self.far = sorted(self.order, key=lambda k: (-k.bit_length(), k))

    def step(self, k, sign):
        if self.half & (self.half - 1):
            return lax.rem(self.z + sign * k + self.half, self.half)
        out = self.z
        for j in range(k.bit_length()):
            if k >> j & 1:
                bit = lax.rem(lax.div(self.z, 1 << j), 2)
                out = out + (1 - 2 * bit) * (1 << j)
        return out

    def to(self, k):
        return self.step(k, 1)

    def frm(self, k):
        return self.step(k, -1)

    def device(self, z):
        return 2 * z + self.y

    def opposite(self, z):
        return 2 * z + 1 - self.y

    def greet(self):
        barrier = pltpu.get_barrier_semaphore()
        n = 2 * self.half
        for k in range(1, n):
            peer = lax.rem(self.me + k, n)
            pl.semaphore_signal(
                barrier, inc=1, device_id={"seq": peer}, device_id_type=MESH
            )
        return lambda: pl.semaphore_wait(barrier, n - 1)


def push(peer, src, dst, send_sem, recv_sem):
    return pltpu.make_async_remote_copy(
        src_ref=src,
        dst_ref=dst,
        send_sem=send_sem,
        recv_sem=recv_sem,
        device_id={"seq": peer},
        device_id_type=MESH,
    )


def index_row(n, b, gq, giw, kbuf, length, store):
    me = lax.axis_index("seq")
    heads, held, span = gq.shape[2], giw.shape[2], kbuf.shape[1]
    tile = min(512, span)
    group = 8
    lane = lax.broadcasted_iota(jnp.int32, (1, tile), 1)
    diagonal = (
        lax.broadcasted_iota(jnp.int32, (n * group, held), 0) % group
        == lax.broadcasted_iota(jnp.int32, (n * group, held), 1)
    )
    low = lax.broadcasted_iota(jnp.int32, (n * group, LANES), 1) < LANES // 2
    packed = gq[:, b, :, LATENT_WIDTH:PACKED].astype(jnp.float32)
    if heads == 2 * group:
        left = packed[:, :group].reshape(n * group, LANES)
        right = packed[:, group:].reshape(n * group, LANES)
    else:
        left = packed.reshape(n * group, LANES)
        right = pltpu.roll(left, n * group - held, 0)
    query = jnp.where(low, pltpu.roll(left, LANES // 2, 1), right)
    query = query.astype(jnp.bfloat16)
    weight = giw[:, b : b + 1].astype(jnp.float32)
    weight = jnp.broadcast_to(weight, (n, group, held)).reshape(n * group, held)
    weight = jnp.sum(jnp.where(diagonal, weight, 0.0), axis=1, keepdims=True)
    weight = jnp.broadcast_to(weight * IDX_DIM ** (-0.5), (n * group, LANES))

    def step(c, carry):
        start = pl.multiple_of(c * tile, tile)
        dots = lax.dot_general(
            query,
            kbuf[b, pl.ds(start, tile), :],
            (((1,), (1,)), ((), ())),
            preferred_element_type=jnp.float32,
        )
        pieces = []
        for j in range(tile // LANES):
            part = jnp.maximum(dots[:, j * LANES : (j + 1) * LANES], 0.0) * weight
            pieces.append(jnp.sum(part, axis=0, keepdims=True))
        total = jnp.concatenate(pieces, axis=1)
        live = me * span + c * tile + lane < length
        store(pl.ds(start, tile), jnp.where(live, total, 0.0))
        return carry

    lax.fori_loop(0, span // tile, step, 0)


def gather_kernel(
    n, lq, iq, iw, sel, lens, cache, keys, weight, gq, giw, cbuf, kbuf, wbuf, table, scores,
    lqs, iqs, sels, ends, load_sem, zsend, zrecv, ysend, yrecv,
):
    line = Line(n)
    me = line.me
    rows, heads, width = lqs.shape
    held = iw.shape[1]
    loads = [
        pltpu.make_async_copy(lq, lqs, load_sem.at[0]),
        pltpu.make_async_copy(iq, iqs, load_sem.at[1]),
        pltpu.make_async_copy(iw, giw.at[me], load_sem.at[2]),
        pltpu.make_async_copy(sel, sels, load_sem.at[3]),
        pltpu.make_async_copy(lens, ends, load_sem.at[4]),
        pltpu.make_async_copy(keys, kbuf, load_sem.at[5]),
        pltpu.make_async_copy(weight, wbuf, load_sem.at[6]),
    ]
    strips = cbuf.shape[1]
    for b in range(rows):
        for j in range(strips):
            loads.append(
                pltpu.make_async_copy(
                    cache.at[b, :, pl.ds(j * STRIP, STRIP)],
                    cbuf.at[b, j],
                    load_sem.at[7 + b * strips + j],
                )
            )
    for copy in loads[:5]:
        copy.start()
    entered = line.greet()
    for copy in loads[:3]:
        copy.wait()

    lane = lax.broadcasted_iota(jnp.int32, (iqs.shape[1], LANES), 1)
    row = lax.broadcasted_iota(jnp.int32, (iqs.shape[1], LANES), 0)
    for b in range(rows):
        mine = iqs[b].astype(jnp.float32)
        turned = pltpu.roll(mine, LANES // 2, 1)
        if heads == 2 * iqs.shape[1]:
            spare = jnp.concatenate([turned, mine], axis=0)
        else:
            spare = jnp.where(row < held, turned, pltpu.roll(mine, held, 0))
        gq[me, b, :, 0:LATENT_WIDTH] = lqs[b, :, 0:LATENT_WIDTH]
        gq[me, b, :, LATENT_WIDTH:width] = lqs[b, :, LATENT_WIDTH:width]
        spare = spare.astype(jnp.bfloat16)
        gq[me, b, :, width:PACKED] = spare[:, width - LATENT_WIDTH :]
    entered()

    def piece(owner, r):
        return gq.at[owner, r] if r < rows else giw.at[owner]

    relayed = (0,) if line.half == 4 else ()
    turns = [0, rows] + list(range(1, rows))
    across, along, onward, relay = {}, {}, {}, {}
    for r in turns:
        ref = piece(me, r)
        across[r] = push(line.partner, ref, ref, ysend.at[0, r], yrecv.at[0, r])
        for k in line.order:
            ref = piece(me, r)
            if r in relayed and k == 3:
                ref = piece(line.device(line.frm(2)), r)
                target = line.device(line.to(1))
            else:
                target = line.device(line.to(k))
            along[k, r] = push(target, ref, ref, zsend.at[k, r], zrecv.at[k, r])
            ref = piece(line.device(line.frm(k)), r)
            onward[k, r] = push(line.partner, ref, ref, ysend.at[k, r], yrecv.at[k, r])
    for r in turns:
        across[r].start()
    for r in turns:
        for k in line.order:
            if not (r in relayed and k == 3):
                along[k, r].start()
    for copy in loads[5:]:
        copy.start()

    for copy in loads[3:5]:
        copy.wait()
    first = me * (keys.shape[1] // BLOCK)
    here = keys.shape[1] // BLOCK
    chosen = sels[...]
    spots = lax.broadcasted_iota(jnp.int32, table.shape, 2)
    which = lax.broadcasted_iota(jnp.int32, table.shape, 0)
    kept = jnp.zeros(table.shape, jnp.int32)
    counts = [jnp.zeros(table.shape, jnp.int32)] * 2
    for i in range(sels.shape[2]):
        block = jnp.broadcast_to(chosen[:, :, i : i + 1], table.shape)
        mine = (block >= first) & (block < first + here)
        odd = block & 1
        for part in range(2):
            take = mine & (odd == part)
            kept = jnp.where(take & (spots == part * SLOTS + counts[part]), block, kept)
            counts[part] = counts[part] + jnp.where(take, 1, 0)
    for b in range(rows):
        kept = jnp.where((spots == LANES - 3) & (which == b), ends[b], kept)
    kept = jnp.where(spots == LANES - 2, counts[0], kept)
    table[...] = jnp.where(spots == LANES - 1, counts[1], kept)

    for r in turns:
        for k in line.order:
            if not (r in relayed and k == 3):
                along[k, r].wait_recv()
                onward[k, r].start()
                if r in relayed and k == 2:
                    along[3, r].start()
    for r in relayed:
        along[3, r].wait_recv()
        onward[3, r].start()

    def complete(r):
        across[r].wait_recv()
        for k in line.order:
            onward[k, r].wait_recv()

    loads[5].wait()
    complete(rows)
    for b in range(rows):
        complete(b)
        if b < EARLY:

            def store(window, value, b=b):
                scores[b : b + 1, window] = value

            index_row(n, b, gq, giw, kbuf, ends[b], store)
    for copy in loads[6:]:
        copy.wait()
    for group in (across, along, onward):
        for copy in group.values():
            copy.wait_send()


def tiles_of(table, cache, b, g, base, tiles):
    rows, strips, width, strip = cache.shape
    first = lax.axis_index("seq") * (strips * strip // BLOCK)
    lane = lax.broadcasted_iota(jnp.int32, (1, LANES), 1)
    keys, bias = [], []
    for j in range(tiles):
        halves, ends = [], []
        for part in range(2):
            held = base + j < table[b, g, LANES - 2 + part]
            block = table[b, g, part * SLOTS + base + j]
            tile = jnp.where(held, (block - first) // 2, 0)
            halves.append(cache[b, tile])
            live = jnp.minimum(BLOCK, table[b, g, LANES - 3] - block * BLOCK)
            ends.append(part * BLOCK + jnp.where(held, live, 0))
        usable = (lane < ends[0]) | ((lane >= BLOCK) & (lane < ends[1]))
        low, high = halves
        keys.append(jnp.concatenate([low[:, :BLOCK], high[:, BLOCK:]], axis=1))
        bias.append(jnp.where(usable, 0.0, NEG))
    return jnp.concatenate(keys, axis=1), jnp.concatenate(bias, axis=1)


def query_of(gq, b, g, width):
    n, _, heads, _ = gq.shape
    per_group = n // HEAD_GROUPS
    query = gq[pl.ds(g * per_group, per_group), b]
    if heads % 16:
        query = query.astype(jnp.float32)
    return query.reshape(per_group * heads, PACKED)[:, :width].astype(jnp.bfloat16)


def scores_of(query, keys, bias):
    scale = (VALUE_WIDTH + ROTARY_WIDTH) ** (-0.5) * LOG2E
    return jnp.dot(query, keys, preferred_element_type=jnp.float32) * scale + bias


def absorb(state, s, keys):
    top, total, acc = state
    new = jnp.maximum(top, jnp.max(s, axis=1, keepdims=True))
    p = jnp.exp2(s - new)
    keep = jnp.exp2(top - new)
    mixed = lax.dot_general(
        p.astype(jnp.bfloat16),
        keys[:LATENT_WIDTH],
        (((1,), (1,)), ((), ())),
        preferred_element_type=jnp.float32,
    )
    return new, total * keep + jnp.sum(p, axis=1, keepdims=True), acc * keep + mixed


def surplus_kernel(table, gq, cache, accs, norms):
    rows, _, width, _ = cache.shape
    wide = accs.shape[1]
    lane = lax.broadcasted_iota(jnp.int32, (1, LANES), 1)

    @pl.loop(0, rows)
    def _(b):
        for g in range(HEAD_GROUPS):
            tiles = jnp.maximum(table[b, g, LANES - 2], table[b, g, LANES - 1])
            steps = (jnp.maximum(tiles - FIRST, 0) + MORE - 1) // MORE

            def more(c, state, g=g):
                keys, bias = tiles_of(table, cache, b, g, FIRST + c * MORE, MORE)
                return absorb(state, scores_of(query_of(gq, b, g, width), keys, bias), keys)

            start = (
                jnp.full((wide, 1), NEG, jnp.float32),
                jnp.zeros((wide, 1), jnp.float32),
                jnp.zeros((wide, LATENT_WIDTH), jnp.float32),
            )
            top, total, acc = lax.fori_loop(0, steps, more, start)
            accs[b * HEAD_GROUPS + g] = acc
            norms[b * HEAD_GROUPS + g] = jnp.where(lane == 0, top, total)


def attend_kernel(
    n, slots, gq, giw, cache, kbuf, accs, norms, scores_in, attended, scores,
    table, own, sent, from_pair, joint, from_line, lse, lses, share,
    slot_sem, ysend, yrecv, zsend, zrecv, lsend, lrecv,
):
    line = Line(n)
    half, me = line.half, line.me
    _, rows, heads, latent = own.shape
    width = cache.shape[2]
    per_group = n // HEAD_GROUPS
    wide = per_group * heads
    fetch = pltpu.make_async_copy(slots, table, slot_sem.at[0])
    fetch.start()
    entered = line.greet()
    fetch.wait()
    even = line.y == 0
    head = lax.broadcasted_iota(jnp.int32, (wide, LANES), 0)
    spot = lax.broadcasted_iota(jnp.int32, (wide, LANES), 1)
    ring = line.far + [0]

    def told(k, b):
        return push(
            lax.rem(me + k, n), lse.at[b], lses.at[me, b], lsend.at[k, b], lrecv.at[k, b]
        )

    def across(k, b):
        z = line.to(k)
        return push(
            line.partner, sent.at[z, b], from_pair.at[z, b], ysend.at[k, b], yrecv.at[k, b]
        )

    def along(k, b):
        z = line.to(k)
        return push(
            line.device(z), joint.at[z, b], from_line.at[line.z, b],
            zsend.at[k, b], zrecv.at[k, b],
        )

    @pl.loop(0, rows)
    def _(b):
        loaded = []
        for g in range(HEAD_GROUPS):
            keys, bias = tiles_of(table, cache, b, g, 0, FIRST)
            loaded.append((scores_of(query_of(gq, b, g, width), keys, bias), keys))
        lses_now = jnp.zeros((1, LANES), jnp.float32)
        for g, (s, keys) in enumerate(loaded):
            norm = norms[b * HEAD_GROUPS + g]
            state = (norm[:, 0:1], norm[:, 1:2], accs[b * HEAD_GROUPS + g])
            top, total, acc = absorb(state, s, keys)
            acc = (acc * (1.0 / total)).reshape(per_group // 2, 2, heads, latent)
            part = jnp.broadcast_to(top + jnp.log2(total), (wide, LANES))
            part = jnp.where(spot == head + g * wide, part, 0.0)
            lses_now += jnp.sum(part, axis=0, keepdims=True)
            here_z = pl.ds(g * per_group // 2, per_group // 2)
            own[here_z, b] = jnp.where(even, acc[:, 0], acc[:, 1])
            sent[here_z, b] = jnp.where(even, acc[:, 1], acc[:, 0]).astype(jnp.bfloat16)
        lse[b] = lses_now
        lses[me, b] = lses_now

        @pl.when(b == 0)
        def _():
            entered()

        for k in range(1, n):
            told(k, b).start()
        for k in ring:
            across(k, b).start()

    @pl.loop(0, rows)
    def _(b):
        for k in range(1, n):
            told(k, b).wait_recv()
        parts = [lses[s, b] for s in range(n)]
        best = functools.reduce(jnp.maximum, parts)
        whole = functools.reduce(jnp.add, [jnp.exp2(part - best) for part in parts])
        best = best + jnp.log2(whole)
        both = [jnp.exp2(lses[me, b] - best), jnp.exp2(lses[line.partner, b] - best)]
        share[...] = jnp.transpose(jnp.concatenate(both * 4, axis=0))
        for k in ring:
            z = line.to(k)
            target = line.device(z)
            part = share[pl.ds(pl.multiple_of(target * heads, heads), heads)]
            across(k, b).wait_recv()
            value = part[:, 0:1] * own[z, b]
            value += part[:, 1:2] * from_pair[z, b].astype(jnp.float32)
            if k:
                joint[z, b] = value.astype(jnp.bfloat16)
            else:
                own[z, b] = value
        for k in line.far:
            along(k, b).start()

    scores[0:EARLY] = scores_in[...]
    for b in range(EARLY, rows):

        def store(window, value, b=b):
            scores[b : b + 1, window] = value

        index_row(n, b, gq, giw, kbuf, table[b, 0, LANES - 3], store)

    @pl.loop(0, rows)
    def _(b):
        value = own[line.z, b]
        for k in line.far:
            along(k, b).wait_recv()
            value += from_line[line.frm(k), b].astype(jnp.float32)
        attended[b] = value.astype(attended.dtype)

    @pl.loop(0, rows)
    def _(b):
        for k in range(1, n):
            told(k, b).wait_send()
        for k in ring:
            across(k, b).wait_send()
        for k in line.far:
            along(k, b).wait_send()


def project_kernel(attended, weight, scores, out, scores_out, sem):
    copy = pltpu.make_async_copy(scores, scores_out, sem.at[0])
    copy.start()
    rows, heads, latent = attended.shape
    flat = attended[...]
    if heads % 16:
        flat = flat.astype(jnp.float32)
    flat = flat.reshape(rows * heads, latent).astype(jnp.bfloat16)
    which = lax.broadcasted_iota(jnp.int32, (rows * heads, 1), 0) % heads
    y = jnp.zeros((rows * heads, weight.shape[2]), jnp.float32)
    for h in range(heads):
        part = jnp.dot(flat, weight[h], preferred_element_type=jnp.float32)
        y = jnp.where(which == h, part, y)
    out[...] = y.reshape(rows, heads, weight.shape[2]).astype(out.dtype)
    copy.wait()


def on_device(
    n,
    latent_cache,
    index_keys,
    latent_query,
    index_query,
    index_weight,
    value_up_weight,
    selected,
    lengths,
):
    cache, keys, lq = latent_cache[0], index_keys[0], latent_query[0]
    iq, iw, weight, sel = index_query[0], index_weight[0], value_up_weight[0], selected[0]
    rows, span, width = cache.shape
    heads = lq.shape[1]
    half = n // 2
    extra = -iq.shape[1] % 8
    if extra:
        iq = jnp.pad(iq, ((0, 0), (0, extra), (0, 0)))
    vmem = pl.BlockSpec(memory_space=pltpu.VMEM)
    smem = pl.BlockSpec(memory_space=pltpu.SMEM)
    hbm = pl.BlockSpec(memory_space=pl.ANY)
    dma = pltpu.SemaphoreType.DMA

    def far(x):
        return pltpu.with_memory_space_constraint(x, pltpu.HBM)

    def near(x):
        return pltpu.with_memory_space_constraint(x, pltpu.VMEM)

    params = functools.partial(pltpu.CompilerParams, vmem_limit_bytes=16 * MIB)
    gq, giw, cbuf, kbuf, wbuf, table, scores = pl.pallas_call(
        functools.partial(gather_kernel, n),
        out_shape=(
            pltpu.VMEM((n, rows, heads, PACKED), lq.dtype),
            pltpu.VMEM((n,) + iw.shape, iw.dtype),
            pltpu.VMEM((rows, span // STRIP, width, STRIP), cache.dtype),
            pltpu.VMEM(keys.shape, keys.dtype),
            pltpu.VMEM(weight.shape, weight.dtype),
            pltpu.VMEM((rows, HEAD_GROUPS, LANES), jnp.int32),
            pltpu.VMEM((EARLY, span), jnp.float32),
        ),
        in_specs=[hbm] * 8,
        out_specs=(vmem,) * 7,
        scratch_shapes=[
            pltpu.VMEM(lq.shape, lq.dtype),
            pltpu.VMEM(iq.shape, iq.dtype),
            pltpu.VMEM(sel.shape, sel.dtype),
            pltpu.SMEM(lengths.shape, lengths.dtype),
            dma((7 + rows * (span // STRIP),)),
            dma((half, rows + 1)), dma((half, rows + 1)),
            dma((half, rows + 1)), dma((half, rows + 1)),
        ],
        compiler_params=params(collective_id=0, has_side_effects=True),
        name="gather",
    )(
        far(lq), far(iq), far(iw), far(sel), far(lengths),
        far(jnp.swapaxes(cache, 1, 2)), far(keys), far(weight),
    )

    pairs = rows * HEAD_GROUPS
    wide = n // HEAD_GROUPS * heads
    accs, norms = pl.pallas_call(
        surplus_kernel,
        out_shape=(
            pltpu.VMEM((pairs, wide, LATENT_WIDTH), jnp.float32),
            pltpu.VMEM((pairs, wide, LANES), jnp.float32),
        ),
        in_specs=[smem, vmem, vmem],
        out_specs=(vmem,) * 2,
        compiler_params=params(),
        name="surplus",
    )(table, near(gq), near(cbuf))

    parts = (half, rows, heads, LATENT_WIDTH)
    attended, scores = pl.pallas_call(
        functools.partial(attend_kernel, n),
        out_shape=(
            pltpu.VMEM((rows, heads, LATENT_WIDTH), jnp.bfloat16),
            pltpu.VMEM((rows, span), jnp.float32),
        ),
        in_specs=[vmem] * 8,
        out_specs=(vmem, vmem),
        scratch_shapes=[
            pltpu.SMEM(table.shape, table.dtype),
            pltpu.VMEM(parts, jnp.float32),
            pltpu.VMEM(parts, jnp.bfloat16),
            pltpu.VMEM(parts, jnp.bfloat16),
            pltpu.VMEM(parts, jnp.bfloat16),
            pltpu.VMEM(parts, jnp.bfloat16),
            pltpu.VMEM((rows, 1, n * heads), jnp.float32),
            pltpu.VMEM((n, rows, 1, n * heads), jnp.float32),
            pltpu.VMEM((n * heads, 8), jnp.float32),
            dma((1,)),
            dma((half, rows)), dma((half, rows)), dma((half, rows)), dma((half, rows)),
            dma((n, rows)), dma((n, rows)),
        ],
        compiler_params=params(collective_id=1, has_side_effects=True),
        name="attend",
    )(
        near(table), near(gq), near(giw), near(cbuf), near(kbuf),
        near(accs), near(norms), near(scores),
    )

    head_out, index_scores = pl.pallas_call(
        project_kernel,
        out_shape=(
            jax.ShapeDtypeStruct((rows, heads, weight.shape[2]), jnp.bfloat16),
            jax.ShapeDtypeStruct((rows, span), jnp.float32),
        ),
        in_specs=[vmem, vmem, vmem],
        out_specs=(vmem, hbm),
        scratch_shapes=[dma((1,))],
        compiler_params=pltpu.CompilerParams(vmem_limit_bytes=16 * MIB),
        name="project",
    )(near(attended), near(wbuf), near(scores))
    return (index_scores[None], head_out[None])


def solution(mesh):
    return jax.shard_map(
        functools.partial(on_device, mesh.shape["seq"]),
        mesh=mesh,
        in_specs=(
            P("section", "groups", "seq", None),
            P("section", "groups", "seq", None),
            P("section", "groups", "seq", None),
            P("section", "groups", "seq", None),
            P("section", "groups", "seq"),
            P("section", "seq", None, None),
            P("section", "groups", None, None),
            P("groups"),
        ),
        out_specs=(P("section", "groups", "seq"), P("section", "groups", "seq", None)),
        check_vma=False,
    )
```

time: 39.1 us -> 40.3 us (1.031); the launches traced: 39.5 us -> 40.2 us
  Pallas kernels: 38.8 us -> 39.5 us
    pallas_call x1, Pallas kernels: 18.4 us -> 21.3 us  [on_device(): pl.pallas_call(functools.partial(gather_kernel, n), out_shape=(pltpu.VMEM...]
    pallas_call x2, Pallas kernels: 18.8 us -> 16.7 us  [the longest x1 15.9 us: on_device(): pl.pallas_call(functools.partial(attend_kernel, n), out_shape=(pltpu.VMEM...]
where the time goes in v4:
time: 40.3 us; the launch traced here: 40.2 us
  Pallas kernels  39.5 us (98%)
  between operations  0.66 us (2%)
    pallas_call x1, Pallas kernels, on_device(): pl.pallas_call(functools.partial(gather_kernel, n), out_shape=(pltpu.VMEM...  21.3 us
    pallas_call x1, Pallas kernels, on_device(): pl.pallas_call(functools.partial(attend_kernel, n), out_shape=(pltpu.VMEM...  15.9 us
    pallas_call x1, Pallas kernels, on_device(): pl.pallas_call(project_kernel, out_shape=(jax.ShapeDtypeStruct((rows, hea...  1.54 us
    pallas_call x1, Pallas kernels, on_device(): pl.pallas_call(surplus_kernel, out_shape=(pltpu.VMEM((pairs, wide, LATENT...  0.81 us

profile of v4, /device:TPU:0, one launch (start us, length us, event | category | flops | bytes accessed | tf_op | source)
XLA Modules:
  0.0 40.2 jit_solution(2665642333943191171)
XLA Ops:
  0.6 21.3 %gather.1 = (bf16[8,4,16,640]{3,2,1,0:T(8,128)(2,1)S(1)}, bf16[8,4,8]{2,1,0:T(4,128)(2,1)S(1)}, bf16[4,32,576,128]{3,2,1,0:T(8,128)(2,1)S(1)}, bf16[4,4096,128]{...) custom-call(bf16[4,16,576]{2,1,0:T(8,128)(2,1)} %bitcast.14, ...), custom_call_target="tpu_custom_call" | custom-call | tf_op jit(solution)/shard_map/gather/pallas_call | solution.py:499
  21.9 0.8 %surplus.1 = (f32[8,64,512]{2,1,0:T(8,128)S(1)}, f32[8,64,128]{2,1,0:T(8,128)S(1)}) custom-call(s32[4,2,128]{2,1,0:T(2,128)S(1)} %get-tuple-element.15.table.slots, bf16[8,4,16,640]{3,2,1,0:T(8,128)(2,1)S(1)} %get-tuple-element.16.gq, bf16[4,32,576,128]{3,2,1,0:T(8,128)(2,1)S(1)} %get-tuple-element.18.cache), custom_call_target="tpu_custom_call" | custom-call | tf_op jit(solution)/shard_map/surplus/pallas_call | solution.py:530
  22.7 15.9 %attend.1 = (bf16[4,16,512]{2,1,0:T(8,128)(2,1)S(1)}, f32[4,4096]{1,0:T(4,128)S(1)}) custom-call(s32[4,2,128]{2,1,0:T(2,128)S(1)} %get-tuple-element.15.table.slots, bf16[8,4,16,640]{3,2,1,0:T(8,128)(2,1)S(1)} %get-tuple-element.16.gq, bf16[8,4,8]{2,1,0:T(4,128)(2,1)S(1)} %get-tuple-element.17.giw, bf16[4,32,576,128]{3,2,1,0:T(8,128)(2,1)S(1)} %get-tuple-element.18.cache, ...), custom_call_target="tpu_custom_call" | custom-call | tf_op jit(solution)/shard_map/attend/pallas_call | solution.py:543
  38.6 1.5 %project.1 = (bf16[4,16,128]{2,1,0:T(8,128)(2,1)}, f32[4,4096]{1,0:T(4,128)}) custom-call(bf16[4,16,512]{2,1,0:T(8,128)(2,1)S(1)} %get-tuple-element.23.attended, bf16[16,512,128]{2,1,0:T(8,128)(2,1)S(1)} %get-tuple-element.24.weight, f32[4,4096]{1,0:T(4,128)S(1)} %get-tuple-element.25.scores), custom_call_target="tpu_custom_call" | custom-call | tf_op jit(solution)/shard_map/project/pallas_call | solution.py:572

commit v5 on v4

--- a/solution.py
+++ b/solution.py
@@ -18,7 +18,6 @@
 FIRST = 4
 MORE = 2
 STRIP = 128
-EARLY = 2
 SLOTS = 62
 LANES = 128
 PACKED = LATENT_WIDTH + LANES
@@ -126,7 +125,7 @@
 
 
 def gather_kernel(
-    n, lq, iq, iw, sel, lens, cache, keys, weight, gq, giw, cbuf, kbuf, wbuf, table, scores,
+    n, lq, iq, iw, sel, lens, cache, gq, giw, cbuf, table,
     lqs, iqs, sels, ends, load_sem, zsend, zrecv, ysend, yrecv,
 ):
     line = Line(n)
@@ -139,8 +138,6 @@
         pltpu.make_async_copy(iw, giw.at[me], load_sem.at[2]),
         pltpu.make_async_copy(sel, sels, load_sem.at[3]),
         pltpu.make_async_copy(lens, ends, load_sem.at[4]),
-        pltpu.make_async_copy(keys, kbuf, load_sem.at[5]),
-        pltpu.make_async_copy(weight, wbuf, load_sem.at[6]),
     ]
     strips = cbuf.shape[1]
     for b in range(rows):
@@ -149,7 +146,7 @@
                 pltpu.make_async_copy(
                     cache.at[b, :, pl.ds(j * STRIP, STRIP)],
                     cbuf.at[b, j],
-                    load_sem.at[7 + b * strips + j],
+                    load_sem.at[5 + b * strips + j],
                 )
             )
     for copy in loads[:5]:
@@ -203,8 +200,8 @@
 
     for copy in loads[3:5]:
         copy.wait()
-    first = me * (keys.shape[1] // BLOCK)
-    here = keys.shape[1] // BLOCK
+    here = strips * STRIP // BLOCK
+    first = me * here
     chosen = sels[...]
     spots = lax.broadcasted_iota(jnp.int32, table.shape, 2)
     which = lax.broadcasted_iota(jnp.int32, table.shape, 0)
@@ -239,17 +236,9 @@
         for k in line.order:
             onward[k, r].wait_recv()
 
-    loads[5].wait()
-    complete(rows)
-    for b in range(rows):
-        complete(b)
-        if b < EARLY:
-
-            def store(window, value, b=b):
-                scores[b : b + 1, window] = value
-
-            index_row(n, b, gq, giw, kbuf, ends[b], store)
-    for copy in loads[6:]:
+    for r in turns:
+        complete(r)
+    for copy in loads[5:]:
         copy.wait()
     for group in (across, along, onward):
         for copy in group.values():
@@ -292,23 +281,27 @@
 
 
 def absorb(state, s, keys):
-    top, total, acc = state
-    new = jnp.maximum(top, jnp.max(s, axis=1, keepdims=True))
+    new = jnp.max(s, axis=1, keepdims=True)
+    if state is not None:
+        new = jnp.maximum(state[0], new)
     p = jnp.exp2(s - new)
-    keep = jnp.exp2(top - new)
     mixed = lax.dot_general(
         p.astype(jnp.bfloat16),
         keys[:LATENT_WIDTH],
         (((1,), (1,)), ((), ())),
         preferred_element_type=jnp.float32,
     )
-    return new, total * keep + jnp.sum(p, axis=1, keepdims=True), acc * keep + mixed
+    whole = jnp.sum(p, axis=1, keepdims=True)
+    if state is None:
+        return new, whole, mixed
+    top, total, acc = state
+    keep = jnp.exp2(top - new)
+    return new, total * keep + whole, acc * keep + mixed
 
 
 def surplus_kernel(table, gq, cache, accs, norms):
     rows, _, width, _ = cache.shape
     wide = accs.shape[1]
-    lane = lax.broadcasted_iota(jnp.int32, (1, LANES), 1)
 
     @pl.loop(0, rows)
     def _(b):
@@ -327,12 +320,13 @@
             )
             top, total, acc = lax.fori_loop(0, steps, more, start)
             accs[b * HEAD_GROUPS + g] = acc
-            norms[b * HEAD_GROUPS + g] = jnp.where(lane == 0, top, total)
+            norms[b * HEAD_GROUPS + g, 0] = jnp.broadcast_to(top, (wide, LANES))
+            norms[b * HEAD_GROUPS + g, 1] = jnp.broadcast_to(total, (wide, LANES))
 
 
 def attend_kernel(
-    n, slots, gq, giw, cache, kbuf, accs, norms, scores_in, attended, scores,
-    table, own, sent, from_pair, joint, from_line, lse, lses, share,
+    n, slots, gq, giw, cache, accs, norms, keys, weight, attended, scores, wbuf,
+    kbuf, table, own, sent, from_pair, joint, from_line, lse, lses, share,
     slot_sem, ysend, yrecv, zsend, zrecv, lsend, lrecv,
 ):
     line = Line(n)
@@ -342,8 +336,12 @@
     per_group = n // HEAD_GROUPS
     wide = per_group * heads
     fetch = pltpu.make_async_copy(slots, table, slot_sem.at[0])
+    key_load = pltpu.make_async_copy(keys, kbuf, slot_sem.at[1])
+    weight_load = pltpu.make_async_copy(weight, wbuf, slot_sem.at[2])
     fetch.start()
     entered = line.greet()
+    key_load.start()
+    weight_load.start()
     fetch.wait()
     even = line.y == 0
     head = lax.broadcasted_iota(jnp.int32, (wide, LANES), 0)
@@ -376,11 +374,22 @@
             loaded.append((scores_of(query_of(gq, b, g, width), keys, bias), keys))
         lses_now = jnp.zeros((1, LANES), jnp.float32)
         for g, (s, keys) in enumerate(loaded):
-            norm = norms[b * HEAD_GROUPS + g]
-            state = (norm[:, 0:1], norm[:, 1:2], accs[b * HEAD_GROUPS + g])
-            top, total, acc = absorb(state, s, keys)
-            acc = (acc * (1.0 / total)).reshape(per_group // 2, 2, heads, latent)
-            part = jnp.broadcast_to(top + jnp.log2(total), (wide, LANES))
+            rg = b * HEAD_GROUPS + g
+            top, total, acc = absorb(None, s, keys)
+            top = jnp.broadcast_to(top, (wide, LANES))
+            best = jnp.maximum(top, norms[rg, 0])
+            grown, added = jnp.exp2(top - best), jnp.exp2(norms[rg, 0] - best)
+            total = grown * total + added * norms[rg, 1]
+            scaled = 1.0 / total
+            grown, added = grown * scaled, added * scaled
+            acc = jnp.concatenate(
+                [
+                    acc[:, j : j + LANES] * grown + accs[rg, :, j : j + LANES] * added
+                    for j in range(0, latent, LANES)
+                ],
+                axis=1,
+            ).reshape(per_group // 2, 2, heads, latent)
+            part = best + jnp.log2(total)
             part = jnp.where(spot == head + g * wide, part, 0.0)
             lses_now += jnp.sum(part, axis=0, keepdims=True)
             here_z = pl.ds(g * per_group // 2, per_group // 2)
@@ -398,8 +407,7 @@
         for k in ring:
             across(k, b).start()
 
-    @pl.loop(0, rows)
-    def _(b):
+    def combine(b):
         for k in range(1, n):
             told(k, b).wait_recv()
         parts = [lses[s, b] for s in range(n)]
@@ -422,13 +430,22 @@
         for k in line.far:
             along(k, b).start()
 
-    scores[0:EARLY] = scores_in[...]
-    for b in range(EARLY, rows):
-
-        def store(window, value, b=b):
+    def index(b):
+        def store(window, value):
             scores[b : b + 1, window] = value
 
         index_row(n, b, gq, giw, kbuf, table[b, 0, LANES - 3], store)
+
+    key_load.wait()
+    index(0)
+    for b in range(rows // 2):
+        combine(b)
+    for b in range(1, rows // 2):
+        index(b)
+    for b in range(rows // 2, rows):
+        combine(b)
+    for b in range(rows // 2, rows):
+        index(b)
 
     @pl.loop(0, rows)
     def _(b):
@@ -446,6 +463,7 @@
             across(k, b).wait_send()
         for k in line.far:
             along(k, b).wait_send()
+    weight_load.wait()
 
 
 def project_kernel(attended, weight, scores, out, scores_out, sem):
@@ -496,25 +514,22 @@
         return pltpu.with_memory_space_constraint(x, pltpu.VMEM)
 
     params = functools.partial(pltpu.CompilerParams, vmem_limit_bytes=16 * MIB)
-    gq, giw, cbuf, kbuf, wbuf, table, scores = pl.pallas_call(
+    gq, giw, cbuf, table = pl.pallas_call(
         functools.partial(gather_kernel, n),
         out_shape=(
             pltpu.VMEM((n, rows, heads, PACKED), lq.dtype),
             pltpu.VMEM((n,) + iw.shape, iw.dtype),
             pltpu.VMEM((rows, span // STRIP, width, STRIP), cache.dtype),
-            pltpu.VMEM(keys.shape, keys.dtype),
-            pltpu.VMEM(weight.shape, weight.dtype),
             pltpu.VMEM((rows, HEAD_GROUPS, LANES), jnp.int32),
-            pltpu.VMEM((EARLY, span), jnp.float32),
         ),
-        in_specs=[hbm] * 8,
-        out_specs=(vmem,) * 7,
+        in_specs=[hbm] * 6,
+        out_specs=(vmem,) * 4,
         scratch_shapes=[
             pltpu.VMEM(lq.shape, lq.dtype),
             pltpu.VMEM(iq.shape, iq.dtype),
             pltpu.VMEM(sel.shape, sel.dtype),
             pltpu.SMEM(lengths.shape, lengths.dtype),
-            dma((7 + rows * (span // STRIP),)),
+            dma((5 + rows * (span // STRIP),)),
             dma((half, rows + 1)), dma((half, rows + 1)),
             dma((half, rows + 1)), dma((half, rows + 1)),
         ],
@@ -522,7 +537,7 @@
         name="gather",
     )(
         far(lq), far(iq), far(iw), far(sel), far(lengths),
-        far(jnp.swapaxes(cache, 1, 2)), far(keys), far(weight),
+        far(jnp.swapaxes(cache, 1, 2)),
     )
 
     pairs = rows * HEAD_GROUPS
@@ -531,7 +546,7 @@
         surplus_kernel,
         out_shape=(
             pltpu.VMEM((pairs, wide, LATENT_WIDTH), jnp.float32),
-            pltpu.VMEM((pairs, wide, LANES), jnp.float32),
+            pltpu.VMEM((pairs, 2, wide, LANES), jnp.float32),
         ),
         in_specs=[smem, vmem, vmem],
         out_specs=(vmem,) * 2,
@@ -540,15 +555,17 @@
     )(table, near(gq), near(cbuf))
 
     parts = (half, rows, heads, LATENT_WIDTH)
-    attended, scores = pl.pallas_call(
+    attended, scores, wbuf = pl.pallas_call(
         functools.partial(attend_kernel, n),
         out_shape=(
             pltpu.VMEM((rows, heads, LATENT_WIDTH), jnp.bfloat16),
             pltpu.VMEM((rows, span), jnp.float32),
+            pltpu.VMEM(weight.shape, weight.dtype),
         ),
-        in_specs=[vmem] * 8,
-        out_specs=(vmem, vmem),
+        in_specs=[vmem] * 6 + [hbm] * 2,
+        out_specs=(vmem,) * 3,
         scratch_shapes=[
+            pltpu.VMEM(keys.shape, keys.dtype),
             pltpu.SMEM(table.shape, table.dtype),
             pltpu.VMEM(parts, jnp.float32),
             pltpu.VMEM(parts, jnp.bfloat16),
@@ -558,15 +575,15 @@
             pltpu.VMEM((rows, 1, n * heads), jnp.float32),
             pltpu.VMEM((n, rows, 1, n * heads), jnp.float32),
             pltpu.VMEM((n * heads, 8), jnp.float32),
-            dma((1,)),
+            dma((3,)),
             dma((half, rows)), dma((half, rows)), dma((half, rows)), dma((half, rows)),
             dma((n, rows)), dma((n, rows)),
         ],
         compiler_params=params(collective_id=1, has_side_effects=True),
         name="attend",
     )(
-        near(table), near(gq), near(giw), near(cbuf), near(kbuf),
-        near(accs), near(norms), near(scores),
+        near(table), near(gq), near(giw), near(cbuf), near(accs), near(norms),
+        far(keys), far(weight),
     )
 
     head_out, index_scores = pl.pallas_call(

time: 40.3 us -> 38.5 us (0.955); the launches traced: 40.2 us -> 37.9 us
  Pallas kernels: 39.5 us -> 37.3 us
    pallas_call x1, Pallas kernels: 21.3 us -> 18.1 us  [on_device(): pl.pallas_call(functools.partial(gather_kernel, n), out_shape=(pltpu.VMEM...]
    pallas_call x1, Pallas kernels: 0.81 us -> 2.44 us  [on_device(): pl.pallas_call(surplus_kernel, out_shape=(pltpu.VMEM((pairs, wide, LATENT...]
    pallas_call x1, Pallas kernels: 15.9 us -> 15.2 us  [on_device(): pl.pallas_call(functools.partial(attend_kernel, n), out_shape=(pltpu.VMEM...]
where the time goes in v5:
time: 38.5 us; the launch traced here: 37.9 us
  Pallas kernels  37.3 us (97%)
  between operations  0.65 us (2%)
    pallas_call x1, Pallas kernels, on_device(): pl.pallas_call(functools.partial(gather_kernel, n), out_shape=(pltpu.VMEM...  18.1 us
    pallas_call x1, Pallas kernels, on_device(): pl.pallas_call(functools.partial(attend_kernel, n), out_shape=(pltpu.VMEM...  15.2 us
    pallas_call x1, Pallas kernels, on_device(): pl.pallas_call(surplus_kernel, out_shape=(pltpu.VMEM((pairs, wide, LATENT...  2.44 us
    pallas_call x1, Pallas kernels, on_device(): pl.pallas_call(project_kernel, out_shape=(jax.ShapeDtypeStruct((rows, hea...  1.55 us

profile of v5, /device:TPU:0, one launch (start us, length us, event | category | flops | bytes accessed | tf_op | source)
XLA Modules:
  0.0 37.9 jit_solution(339323847832608193)
XLA Ops:
  0.6 18.1 %gather.1 = (bf16[8,4,16,640]{3,2,1,0:T(8,128)(2,1)S(1)}, bf16[8,4,8]{2,1,0:T(4,128)(2,1)S(1)}, bf16[4,32,576,128]{3,2,1,0:T(8,128)(2,1)S(1)}, s32[4,2,128]{2,1,0:T(2,128)S(1)}) custom-call(bf16[4,16,576]{2,1,0:T(8,128)(2,1)} %bitcast.14, bf16[4,8,128]{2,1,0:T(8,128)(2,1)} %bitcast.15, bf16[4,8]{1,0:T(4,128)(2,1)} %bitcast.17, s32[4,2,32]{2,1,0:T(2,128)} %bitcast.16, ...), custom_call_target="tpu_custom_call" | custom-call | tf_op jit(solution)/shard_map/gather/pallas_call | solution.py:517
  18.7 2.4 %surplus.1 = (f32[8,64,512]{2,1,0:T(8,128)S(1)}, f32[8,2,64,128]{3,2,1,0:T(8,128)S(1)}) custom-call(s32[4,2,128]{2,1,0:T(2,128)S(1)} %get-tuple-element.13.table.slots, bf16[8,4,16,640]{3,2,1,0:T(8,128)(2,1)S(1)} %get-tuple-element.14.gq, bf16[4,32,576,128]{3,2,1,0:T(8,128)(2,1)S(1)} %get-tuple-element.16.cache), custom_call_target="tpu_custom_call" | custom-call | tf_op jit(solution)/shard_map/surplus/pallas_call | solution.py:545
  21.2 15.2 %attend.1 = (bf16[4,16,512]{2,1,0:T(8,128)(2,1)S(1)}, f32[4,4096]{1,0:T(4,128)S(1)}, bf16[16,512,128]{2,1,0:T(8,128)(2,1)S(1)}) custom-call(s32[4,2,128]{2,1,0:T(2,128)S(1)} %get-tuple-element.13.table.slots, bf16[8,4,16,640]{3,2,1,0:T(8,128)(2,1)S(1)} %get-tuple-element.14.gq, bf16[8,4,8]{2,1,0:T(4,128)(2,1)S(1)} %get-tuple-element.15.giw, ...), custom_call_target="tpu_custom_call" | custom-call | tf_op jit(solution)/shard_map/attend/pallas_call | solution.py:558
  36.4 1.6 %project.1 = (bf16[4,16,128]{2,1,0:T(8,128)(2,1)}, f32[4,4096]{1,0:T(4,128)}) custom-call(bf16[4,16,512]{2,1,0:T(8,128)(2,1)S(1)} %get-tuple-element.19.attended, bf16[16,512,128]{2,1,0:T(8,128)(2,1)S(1)} %get-tuple-element.20.weight, f32[4,4096]{1,0:T(4,128)S(1)} %get-tuple-element.21.scores), custom_call_target="tpu_custom_call" | custom-call | tf_op jit(solution)/shard_map/project/pallas_call | solution.py:589

commit v6 on v5

--- a/solution.py
+++ b/solution.py
@@ -15,7 +15,7 @@
 HEAD_GROUPS = 2
 NEG = -1e30
 LOG2E = 1.4426950408889634
-FIRST = 4
+FIRST = 5
 MORE = 2
 STRIP = 128
 SLOTS = 62
@@ -173,7 +173,7 @@
     def piece(owner, r):
         return gq.at[owner, r] if r < rows else giw.at[owner]
 
-    relayed = (0,) if line.half == 4 else ()
+    relayed = (0, 1) if line.half == 4 else ()
     turns = [0, rows] + list(range(1, rows))
     across, along, onward, relay = {}, {}, {}, {}
     for r in turns:
@@ -402,10 +402,10 @@
         def _():
             entered()
 
+        for k in ring:
+            across(k, b).start()
         for k in range(1, n):
             told(k, b).start()
-        for k in ring:
-            across(k, b).start()
 
     def combine(b):
         for k in range(1, n):
@@ -475,10 +475,13 @@
         flat = flat.astype(jnp.float32)
     flat = flat.reshape(rows * heads, latent).astype(jnp.bfloat16)
     which = lax.broadcasted_iota(jnp.int32, (rows * heads, 1), 0) % heads
+
+    def project(h, y):
+        part = jnp.dot(flat, weight[h], preferred_element_type=jnp.float32)
+        return jnp.where(which == h, part, y)
+
     y = jnp.zeros((rows * heads, weight.shape[2]), jnp.float32)
-    for h in range(heads):
-        part = jnp.dot(flat, weight[h], preferred_element_type=jnp.float32)
-        y = jnp.where(which == h, part, y)
+    y = lax.fori_loop(0, heads, project, y, unroll=8)
     out[...] = y.reshape(rows, heads, weight.shape[2]).astype(out.dtype)
     copy.wait()
 

time: 38.5 us -> 37 us (0.961)
  Pallas kernels: 37.3 us -> 36 us
    pallas_call x1, Pallas kernels: 2.44 us -> 0.82 us  [on_device(): pl.pallas_call(surplus_kernel, out_shape=(pltpu.VMEM((pairs, wide, LATENT...]
    pallas_call x1, Pallas kernels: 15.2 us -> 16.4 us  [on_device(): pl.pallas_call(functools.partial(attend_kernel, n), out_shape=(pltpu.VMEM...]
    pallas_call x1, Pallas kernels: 18.1 us -> 17.5 us  [on_device(): pl.pallas_call(functools.partial(gather_kernel, n), out_shape=(pltpu.VMEM...]
where the time goes in v6:
time: 37 us; the launch traced here: 36.6 us
  Pallas kernels  36 us (97%)
  between operations  0.65 us (2%)
    pallas_call x1, Pallas kernels, on_device(): pl.pallas_call(functools.partial(gather_kernel, n), out_shape=(pltpu.VMEM...  17.5 us
    pallas_call x1, Pallas kernels, on_device(): pl.pallas_call(functools.partial(attend_kernel, n), out_shape=(pltpu.VMEM...  16.4 us
    pallas_call x1, Pallas kernels, on_device(): pl.pallas_call(project_kernel, out_shape=(jax.ShapeDtypeStruct((rows, hea...  1.24 us
    pallas_call x1, Pallas kernels, on_device(): pl.pallas_call(surplus_kernel, out_shape=(pltpu.VMEM((pairs, wide, LATENT...  0.82 us

profile of v6, /device:TPU:0, one launch (start us, length us, event | category | flops | bytes accessed | tf_op | source)
XLA Modules:
  0.0 36.6 jit_solution(11318839187363236385)
XLA Ops:
  0.6 17.5 %gather.1 = (bf16[8,4,16,640]{3,2,1,0:T(8,128)(2,1)S(1)}, bf16[8,4,8]{2,1,0:T(4,128)(2,1)S(1)}, bf16[4,32,576,128]{3,2,1,0:T(8,128)(2,1)S(1)}, s32[4,2,128]{2,1,0:T(2,128)S(1)}) custom-call(bf16[4,16,576]{2,1,0:T(8,128)(2,1)} %bitcast.14, bf16[4,8,128]{2,1,0:T(8,128)(2,1)} %bitcast.15, bf16[4,8]{1,0:T(4,128)(2,1)} %bitcast.17, s32[4,2,32]{2,1,0:T(2,128)} %bitcast.16, ...), custom_call_target="tpu_custom_call" | custom-call | tf_op jit(solution)/shard_map/gather/pallas_call | solution.py:520
  18.2 0.8 %surplus.1 = (f32[8,64,512]{2,1,0:T(8,128)S(1)}, f32[8,2,64,128]{3,2,1,0:T(8,128)S(1)}) custom-call(s32[4,2,128]{2,1,0:T(2,128)S(1)} %get-tuple-element.13.table.slots, bf16[8,4,16,640]{3,2,1,0:T(8,128)(2,1)S(1)} %get-tuple-element.14.gq, bf16[4,32,576,128]{3,2,1,0:T(8,128)(2,1)S(1)} %get-tuple-element.16.cache), custom_call_target="tpu_custom_call" | custom-call | tf_op jit(solution)/shard_map/surplus/pallas_call | solution.py:548
  19.0 16.4 %attend.1 = (bf16[4,16,512]{2,1,0:T(8,128)(2,1)S(1)}, f32[4,4096]{1,0:T(4,128)S(1)}, bf16[16,512,128]{2,1,0:T(8,128)(2,1)S(1)}) custom-call(s32[4,2,128]{2,1,0:T(2,128)S(1)} %get-tuple-element.13.table.slots, bf16[8,4,16,640]{3,2,1,0:T(8,128)(2,1)S(1)} %get-tuple-element.14.gq, bf16[8,4,8]{2,1,0:T(4,128)(2,1)S(1)} %get-tuple-element.15.giw, ...), custom_call_target="tpu_custom_call" | custom-call | tf_op jit(solution)/shard_map/attend/pallas_call | solution.py:561
  35.4 1.2 %project.1 = (bf16[4,16,128]{2,1,0:T(8,128)(2,1)}, f32[4,4096]{1,0:T(4,128)}) custom-call(bf16[4,16,512]{2,1,0:T(8,128)(2,1)S(1)} %get-tuple-element.19.attended, bf16[16,512,128]{2,1,0:T(8,128)(2,1)S(1)} %get-tuple-element.20.weight, f32[4,4096]{1,0:T(4,128)S(1)} %get-tuple-element.21.scores), custom_call_target="tpu_custom_call" | custom-call | tf_op jit(solution)/shard_map/project/pallas_call | solution.py:592

commit v7 on v6

--- a/solution.py
+++ b/solution.py
@@ -15,7 +15,7 @@
 HEAD_GROUPS = 2
 NEG = -1e30
 LOG2E = 1.4426950408889634
-FIRST = 5
+FIRST = 6
 MORE = 2
 STRIP = 128
 SLOTS = 62
@@ -203,22 +203,30 @@
     here = strips * STRIP // BLOCK
     first = me * here
     chosen = sels[...]
-    spots = lax.broadcasted_iota(jnp.int32, table.shape, 2)
-    which = lax.broadcasted_iota(jnp.int32, table.shape, 0)
-    kept = jnp.zeros(table.shape, jnp.int32)
-    counts = [jnp.zeros(table.shape, jnp.int32)] * 2
+    shape = table.shape[1:]
+    spots = lax.broadcasted_iota(jnp.int32, shape, 2)
+    which = lax.broadcasted_iota(jnp.int32, shape, 0)
+    kept = jnp.zeros(shape, jnp.int32)
+    counts = [jnp.zeros(shape, jnp.int32)] * 2
     for i in range(sels.shape[2]):
-        block = jnp.broadcast_to(chosen[:, :, i : i + 1], table.shape)
+        block = jnp.broadcast_to(chosen[:, :, i : i + 1], shape)
         mine = (block >= first) & (block < first + here)
         odd = block & 1
         for part in range(2):
             take = mine & (odd == part)
             kept = jnp.where(take & (spots == part * SLOTS + counts[part]), block, kept)
             counts[part] = counts[part] + jnp.where(take, 1, 0)
+    ends_now = jnp.zeros(spots.shape, jnp.int32)
     for b in range(rows):
-        kept = jnp.where((spots == LANES - 3) & (which == b), ends[b], kept)
-    kept = jnp.where(spots == LANES - 2, counts[0], kept)
-    table[...] = jnp.where(spots == LANES - 1, counts[1], kept)
+        ends_now = jnp.where(which == b, ends[b], ends_now)
+    late = spots >= SLOTS
+    held = spots - jnp.where(late, SLOTS, 0) < jnp.where(late, counts[1], counts[0])
+    live = jnp.minimum(BLOCK, ends_now - kept * BLOCK) + jnp.where(late, BLOCK, 0)
+    table[1] = jnp.where(held, live, 0)
+    tiles = jnp.where(held, (kept - first) >> 1, 0)
+    tiles = jnp.where(spots == LANES - 3, ends_now, tiles)
+    tiles = jnp.where(spots == LANES - 2, counts[0], tiles)
+    table[0] = jnp.where(spots == LANES - 1, counts[1], tiles)
 
     for r in turns:
         for k in line.order:
@@ -246,21 +254,14 @@
 
 
 def tiles_of(table, cache, b, g, base, tiles):
-    rows, strips, width, strip = cache.shape
-    first = lax.axis_index("seq") * (strips * strip // BLOCK)
     lane = lax.broadcasted_iota(jnp.int32, (1, LANES), 1)
     keys, bias = [], []
     for j in range(tiles):
-        halves, ends = [], []
-        for part in range(2):
-            held = base + j < table[b, g, LANES - 2 + part]
-            block = table[b, g, part * SLOTS + base + j]
-            tile = jnp.where(held, (block - first) // 2, 0)
-            halves.append(cache[b, tile])
-            live = jnp.minimum(BLOCK, table[b, g, LANES - 3] - block * BLOCK)
-            ends.append(part * BLOCK + jnp.where(held, live, 0))
-        usable = (lane < ends[0]) | ((lane >= BLOCK) & (lane < ends[1]))
-        low, high = halves
+        even, odd = base + j, SLOTS + base + j
+        low, high = cache[b, table[0, b, g, even]], cache[b, table[0, b, g, odd]]
+        usable = (lane < table[1, b, g, even]) | (
+            (lane >= BLOCK) & (lane < table[1, b, g, odd])
+        )
         keys.append(jnp.concatenate([low[:, :BLOCK], high[:, BLOCK:]], axis=1))
         bias.append(jnp.where(usable, 0.0, NEG))
     return jnp.concatenate(keys, axis=1), jnp.concatenate(bias, axis=1)
@@ -306,7 +307,7 @@
     @pl.loop(0, rows)
     def _(b):
         for g in range(HEAD_GROUPS):
-            tiles = jnp.maximum(table[b, g, LANES - 2], table[b, g, LANES - 1])
+            tiles = jnp.maximum(table[0, b, g, LANES - 2], table[0, b, g, LANES - 1])
             steps = (jnp.maximum(tiles - FIRST, 0) + MORE - 1) // MORE
 
             def more(c, state, g=g):
@@ -416,25 +417,30 @@
         best = best + jnp.log2(whole)
         both = [jnp.exp2(lses[me, b] - best), jnp.exp2(lses[line.partner, b] - best)]
         share[...] = jnp.transpose(jnp.concatenate(both * 4, axis=0))
+        ready = []
         for k in ring:
             z = line.to(k)
             target = line.device(z)
             part = share[pl.ds(pl.multiple_of(target * heads, heads), heads)]
             across(k, b).wait_recv()
+            for copy in ready:
+                copy.start()
             value = part[:, 0:1] * own[z, b]
             value += part[:, 1:2] * from_pair[z, b].astype(jnp.float32)
+            ready = []
             if k:
                 joint[z, b] = value.astype(jnp.bfloat16)
+                ready = [along(k, b)]
             else:
                 own[z, b] = value
-        for k in line.far:
-            along(k, b).start()
+        for copy in ready:
+            copy.start()
 
     def index(b):
         def store(window, value):
             scores[b : b + 1, window] = value
 
-        index_row(n, b, gq, giw, kbuf, table[b, 0, LANES - 3], store)
+        index_row(n, b, gq, giw, kbuf, table[0, b, 0, LANES - 3], store)
 
     key_load.wait()
     index(0)
@@ -523,7 +529,7 @@
             pltpu.VMEM((n, rows, heads, PACKED), lq.dtype),
             pltpu.VMEM((n,) + iw.shape, iw.dtype),
             pltpu.VMEM((rows, span // STRIP, width, STRIP), cache.dtype),
-            pltpu.VMEM((rows, HEAD_GROUPS, LANES), jnp.int32),
+            pltpu.VMEM((2, rows, HEAD_GROUPS, LANES), jnp.int32),
         ),
         in_specs=[hbm] * 6,
         out_specs=(vmem,) * 4,

time: 37 us -> 37 us (level)
  no operation moved by 1% of the time
where the time goes in v7:
time: 37 us
  Pallas kernels  36.3 us (98%)
  between operations  0.66 us (2%)
    pallas_call x1, Pallas kernels, on_device(): pl.pallas_call(functools.partial(gather_kernel, n), out_shape=(pltpu.VMEM...  17.5 us
    pallas_call x1, Pallas kernels, on_device(): pl.pallas_call(functools.partial(attend_kernel, n), out_shape=(pltpu.VMEM...  16.7 us
    pallas_call x1, Pallas kernels, on_device(): pl.pallas_call(project_kernel, out_shape=(jax.ShapeDtypeStruct((rows, hea...  1.24 us
    pallas_call x1, Pallas kernels, on_device(): pl.pallas_call(surplus_kernel, out_shape=(pltpu.VMEM((pairs, wide, LATENT...  0.88 us

profile of v7, /device:TPU:0, one launch (start us, length us, event | category | flops | bytes accessed | tf_op | source)
XLA Modules:
  0.0 37.0 jit_solution(11797570393654437031)
XLA Ops:
  0.6 17.5 %gather.1 = (bf16[8,4,16,640]{3,2,1,0:T(8,128)(2,1)S(1)}, bf16[8,4,8]{2,1,0:T(4,128)(2,1)S(1)}, bf16[4,32,576,128]{3,2,1,0:T(8,128)(2,1)S(1)}, s32[2,4,2,128]{3,2,1,0:T(2,128)S(1)}) custom-call(bf16[4,16,576]{2,1,0:T(8,128)(2,1)} %bitcast.14, bf16[4,8,128]{2,1,0:T(8,128)(2,1)} %bitcast.15, bf16[4,8]{1,0:T(4,128)(2,1)} %bitcast.17, s32[4,2,32]{2,1,0:T(2,128)} %bitcast.16, ...), custom_call_target="tpu_custom_call" | custom-call | tf_op jit(solution)/shard_map/gather/pallas_call | solution.py:526
  18.2 0.9 %surplus.1 = (f32[8,64,512]{2,1,0:T(8,128)S(1)}, f32[8,2,64,128]{3,2,1,0:T(8,128)S(1)}) custom-call(s32[2,4,2,128]{3,2,1,0:T(2,128)S(1)} %get-tuple-element.13.table.slots, bf16[8,4,16,640]{3,2,1,0:T(8,128)(2,1)S(1)} %get-tuple-element.14.gq, bf16[4,32,576,128]{3,2,1,0:T(8,128)(2,1)S(1)} %get-tuple-element.16.cache), custom_call_target="tpu_custom_call" | custom-call | tf_op jit(solution)/shard_map/surplus/pallas_call | solution.py:554
  19.0 16.7 %attend.1 = (bf16[4,16,512]{2,1,0:T(8,128)(2,1)S(1)}, f32[4,4096]{1,0:T(4,128)S(1)}, bf16[16,512,128]{2,1,0:T(8,128)(2,1)S(1)}) custom-call(s32[2,4,2,128]{3,2,1,0:T(2,128)S(1)} %get-tuple-element.13.table.slots, bf16[8,4,16,640]{3,2,1,0:T(8,128)(2,1)S(1)} %get-tuple-element.14.gq, bf16[8,4,8]{2,1,0:T(4,128)(2,1)S(1)} %get-tuple-element.15.giw, ...), custom_call_target="tpu_custom_call" | custom-call | tf_op jit(solution)/shard_map/attend/pallas_call | solution.py:567
  35.7 1.2 %project.1 = (bf16[4,16,128]{2,1,0:T(8,128)(2,1)}, f32[4,4096]{1,0:T(4,128)}) custom-call(bf16[4,16,512]{2,1,0:T(8,128)(2,1)S(1)} %get-tuple-element.19.attended, bf16[16,512,128]{2,1,0:T(8,128)(2,1)S(1)} %get-tuple-element.20.weight, f32[4,4096]{1,0:T(4,128)S(1)} %get-tuple-element.21.scores), custom_call_target="tpu_custom_call" | custom-call | tf_op jit(solution)/shard_map/project/pallas_call | solution.py:598

commit v8 on v7

--- a/solution.py
+++ b/solution.py
@@ -15,7 +15,7 @@
 HEAD_GROUPS = 2
 NEG = -1e30
 LOG2E = 1.4426950408889634
-FIRST = 6
+FIRST = 5
 MORE = 2
 STRIP = 128
 SLOTS = 62
@@ -244,13 +244,15 @@
         for k in line.order:
             onward[k, r].wait_recv()
 
+    for copy in loads[5:]:
+        copy.wait()
+    for group in (across, along):
+        for copy in group.values():
+            copy.wait_send()
     for r in turns:
         complete(r)
-    for copy in loads[5:]:
-        copy.wait()
-    for group in (across, along, onward):
-        for copy in group.values():
-            copy.wait_send()
+    for copy in onward.values():
+        copy.wait_send()
 
 
 def tiles_of(table, cache, b, g, base, tiles):
@@ -455,6 +457,15 @@
 
     @pl.loop(0, rows)
     def _(b):
+        for k in range(1, n):
+            told(k, b).wait_send()
+        for k in ring:
+            across(k, b).wait_send()
+
+    weight_load.wait()
+
+    @pl.loop(0, rows)
+    def _(b):
         value = own[line.z, b]
         for k in line.far:
             along(k, b).wait_recv()
@@ -463,13 +474,8 @@
 
     @pl.loop(0, rows)
     def _(b):
-        for k in range(1, n):
-            told(k, b).wait_send()
-        for k in ring:
-            across(k, b).wait_send()
         for k in line.far:
             along(k, b).wait_send()
-    weight_load.wait()
 
 
 def project_kernel(attended, weight, scores, out, scores_out, sem):

time: 37 us -> 36.3 us (0.981)
  Pallas kernels: 36.3 us -> 35.5 us
    pallas_call x1, Pallas kernels: 16.7 us -> 16.1 us  [on_device(): pl.pallas_call(functools.partial(attend_kernel, n), out_shape=(pltpu.VMEM...]
where the time goes in v8:
time: 36.3 us; the launch traced here: 36.2 us
  Pallas kernels  35.5 us (98%)
  between operations  0.66 us (2%)
    pallas_call x1, Pallas kernels, on_device(): pl.pallas_call(functools.partial(gather_kernel, n), out_shape=(pltpu.VMEM...  17.3 us
    pallas_call x1, Pallas kernels, on_device(): pl.pallas_call(functools.partial(attend_kernel, n), out_shape=(pltpu.VMEM...  16.1 us
    pallas_call x1, Pallas kernels, on_device(): pl.pallas_call(project_kernel, out_shape=(jax.ShapeDtypeStruct((rows, hea...  1.24 us
    pallas_call x1, Pallas kernels, on_device(): pl.pallas_call(surplus_kernel, out_shape=(pltpu.VMEM((pairs, wide, LATENT...  0.88 us

profile of v8, /device:TPU:0, one launch (start us, length us, event | category | flops | bytes accessed | tf_op | source)
XLA Modules:
  0.0 36.2 jit_solution(12264759448895867715)
XLA Ops:
  0.6 17.3 %gather.1 = (bf16[8,4,16,640]{3,2,1,0:T(8,128)(2,1)S(1)}, bf16[8,4,8]{2,1,0:T(4,128)(2,1)S(1)}, bf16[4,32,576,128]{3,2,1,0:T(8,128)(2,1)S(1)}, s32[2,4,2,128]{3,2,1,0:T(2,128)S(1)}) custom-call(bf16[4,16,576]{2,1,0:T(8,128)(2,1)} %bitcast.14, bf16[4,8,128]{2,1,0:T(8,128)(2,1)} %bitcast.15, bf16[4,8]{1,0:T(4,128)(2,1)} %bitcast.17, s32[4,2,32]{2,1,0:T(2,128)} %bitcast.16, ...), custom_call_target="tpu_custom_call" | custom-call | tf_op jit(solution)/shard_map/gather/pallas_call | solution.py:532
  17.9 0.9 %surplus.1 = (f32[8,64,512]{2,1,0:T(8,128)S(1)}, f32[8,2,64,128]{3,2,1,0:T(8,128)S(1)}) custom-call(s32[2,4,2,128]{3,2,1,0:T(2,128)S(1)} %get-tuple-element.13.table.slots, bf16[8,4,16,640]{3,2,1,0:T(8,128)(2,1)S(1)} %get-tuple-element.14.gq, bf16[4,32,576,128]{3,2,1,0:T(8,128)(2,1)S(1)} %get-tuple-element.16.cache), custom_call_target="tpu_custom_call" | custom-call | tf_op jit(solution)/shard_map/surplus/pallas_call | solution.py:560
  18.8 16.1 %attend.1 = (bf16[4,16,512]{2,1,0:T(8,128)(2,1)S(1)}, f32[4,4096]{1,0:T(4,128)S(1)}, bf16[16,512,128]{2,1,0:T(8,128)(2,1)S(1)}) custom-call(s32[2,4,2,128]{3,2,1,0:T(2,128)S(1)} %get-tuple-element.13.table.slots, bf16[8,4,16,640]{3,2,1,0:T(8,128)(2,1)S(1)} %get-tuple-element.14.gq, bf16[8,4,8]{2,1,0:T(4,128)(2,1)S(1)} %get-tuple-element.15.giw, ...), custom_call_target="tpu_custom_call" | custom-call | tf_op jit(solution)/shard_map/attend/pallas_call | solution.py:573
  34.9 1.2 %project.1 = (bf16[4,16,128]{2,1,0:T(8,128)(2,1)}, f32[4,4096]{1,0:T(4,128)}) custom-call(bf16[4,16,512]{2,1,0:T(8,128)(2,1)S(1)} %get-tuple-element.19.attended, bf16[16,512,128]{2,1,0:T(8,128)(2,1)S(1)} %get-tuple-element.20.weight, f32[4,4096]{1,0:T(4,128)S(1)} %get-tuple-element.21.scores), custom_call_target="tpu_custom_call" | custom-call | tf_op jit(solution)/shard_map/project/pallas_call | solution.py:604

commit v9 on v8

--- a/solution.py
+++ b/solution.py
@@ -16,7 +16,7 @@
 NEG = -1e30
 LOG2E = 1.4426950408889634
 FIRST = 5
-MORE = 2
+MORE = 3
 STRIP = 128
 SLOTS = 62
 LANES = 128

time: 36.3 us -> 36.6 us (level)
  Pallas kernels: 35.5 us -> 35.9 us
    pallas_call x1, Pallas kernels: 16.1 us -> 16.5 us  [on_device(): pl.pallas_call(functools.partial(attend_kernel, n), out_shape=(pltpu.VMEM...]
where the time goes in v9:
time: 36.6 us
  Pallas kernels  35.9 us (98%)
  between operations  0.66 us (2%)
    pallas_call x1, Pallas kernels, on_device(): pl.pallas_call(functools.partial(gather_kernel, n), out_shape=(pltpu.VMEM...  17.3 us
    pallas_call x1, Pallas kernels, on_device(): pl.pallas_call(functools.partial(attend_kernel, n), out_shape=(pltpu.VMEM...  16.5 us
    pallas_call x1, Pallas kernels, on_device(): pl.pallas_call(project_kernel, out_shape=(jax.ShapeDtypeStruct((rows, hea...  1.24 us
    pallas_call x1, Pallas kernels, on_device(): pl.pallas_call(surplus_kernel, out_shape=(pltpu.VMEM((pairs, wide, LATENT...  0.94 us

profile of v9, /device:TPU:0, one launch (start us, length us, event | category | flops | bytes accessed | tf_op | source)
XLA Modules:
  0.0 36.6 jit_solution(8022841811263863833)
XLA Ops:
  0.6 17.3 %gather.1 = (bf16[8,4,16,640]{3,2,1,0:T(8,128)(2,1)S(1)}, bf16[8,4,8]{2,1,0:T(4,128)(2,1)S(1)}, bf16[4,32,576,128]{3,2,1,0:T(8,128)(2,1)S(1)}, s32[2,4,2,128]{3,2,1,0:T(2,128)S(1)}) custom-call(bf16[4,16,576]{2,1,0:T(8,128)(2,1)} %bitcast.14, bf16[4,8,128]{2,1,0:T(8,128)(2,1)} %bitcast.15, bf16[4,8]{1,0:T(4,128)(2,1)} %bitcast.17, s32[4,2,32]{2,1,0:T(2,128)} %bitcast.16, ...), custom_call_target="tpu_custom_call" | custom-call | tf_op jit(solution)/shard_map/gather/pallas_call | solution.py:532
  17.9 0.9 %surplus.1 = (f32[8,64,512]{2,1,0:T(8,128)S(1)}, f32[8,2,64,128]{3,2,1,0:T(8,128)S(1)}) custom-call(s32[2,4,2,128]{3,2,1,0:T(2,128)S(1)} %get-tuple-element.13.table.slots, bf16[8,4,16,640]{3,2,1,0:T(8,128)(2,1)S(1)} %get-tuple-element.14.gq, bf16[4,32,576,128]{3,2,1,0:T(8,128)(2,1)S(1)} %get-tuple-element.16.cache), custom_call_target="tpu_custom_call" | custom-call | tf_op jit(solution)/shard_map/surplus/pallas_call | solution.py:560
  18.9 16.5 %attend.1 = (bf16[4,16,512]{2,1,0:T(8,128)(2,1)S(1)}, f32[4,4096]{1,0:T(4,128)S(1)}, bf16[16,512,128]{2,1,0:T(8,128)(2,1)S(1)}) custom-call(s32[2,4,2,128]{3,2,1,0:T(2,128)S(1)} %get-tuple-element.13.table.slots, bf16[8,4,16,640]{3,2,1,0:T(8,128)(2,1)S(1)} %get-tuple-element.14.gq, bf16[8,4,8]{2,1,0:T(4,128)(2,1)S(1)} %get-tuple-element.15.giw, ...), custom_call_target="tpu_custom_call" | custom-call | tf_op jit(solution)/shard_map/attend/pallas_call | solution.py:573
  35.4 1.2 %project.1 = (bf16[4,16,128]{2,1,0:T(8,128)(2,1)}, f32[4,4096]{1,0:T(4,128)}) custom-call(bf16[4,16,512]{2,1,0:T(8,128)(2,1)S(1)} %get-tuple-element.19.attended, bf16[16,512,128]{2,1,0:T(8,128)(2,1)S(1)} %get-tuple-element.20.weight, f32[4,4096]{1,0:T(4,128)S(1)} %get-tuple-element.21.scores), custom_call_target="tpu_custom_call" | custom-call | tf_op jit(solution)/shard_map/project/pallas_call | solution.py:604
